TPU v7x, 32 devices: a whole 2x2x4 slice. The times are simulated.
32 devices in a mesh: dp: 8 (over z, y), neg: 4 (over x, core).
Axes of the slice: x: 2, y: 2, z: 4, core: 2. Of those that a mesh axis runs over, the one named last changes fastest.
Arguments:
- query_features: bfloat16 [8192, 512], P(('dp', 'neg')), may hold values from -8 to 8
- positive_features: bfloat16 [8192, 512], P(('dp', 'neg')), may hold values from -6 to 6
- negative_features: bfloat16 [16384, 512], P(('neg', 'dp')), may hold values from -6 to 6
- positive_ids: int32 [8192], P('dp'), may hold values from 0 to 8191, as said below
- positive_counts: int32 [8192], P(('dp', 'neg')), may hold values from 1 to 16
- negative_ids: int32 [16384], P('neg'), may hold values from 0 to 4095, as said below
- negative_counts: int32 [16384], P('neg'), may hold values from 64 to 4096
- query_first: bfloat16 [512, 1024], replicated, may hold values from -0.25 to 0.25
- query_second: bfloat16 [1024, 512], replicated, may hold values from -0.1875 to 0.1875
- query_third: bfloat16 [512, 256], replicated, may hold values from -0.25 to 0.25
- item_first: bfloat16 [512, 1024], replicated, may hold values from -0.25 to 0.25
- item_second: bfloat16 [1024, 512], replicated, may hold values from -0.1875 to 0.1875
- item_third: bfloat16 [512, 256], replicated, may hold values from -0.25 to 0.25
Outputs:
- mean_loss: float32 [], replicated
- clipped_query_first: float32 [512, 1024], P('dp')
- clipped_query_second: float32 [1024, 512], P('dp')
- clipped_query_third: float32 [512, 256], P('dp')
- clipped_item_first: float32 [512, 1024], P('dp')
- clipped_item_second: float32 [1024, 512], P('dp')
- clipped_item_third: float32 [512, 256], P('dp')
Inputs may be any that keep to these rules, and one draw needn't show every extreme that they name: `negative_ids`: ids of the sampled negatives; one id may stand for several negatives. `positive_ids`: A query's positive id may equal the ids of some negatives; those negatives are left out of that query's denominator.
All inputs are finite; a program needn't handle non-finite values.
Results may differ from a plain program's by a relative error of at most 0.0075.
Values may be sent and summed in bfloat16 or wider, within the bound.
A program may use at most 128 MiB of HBM per device.

v0:
```python
import jax
import jax.numpy as jnp
from jax import lax
from jax.sharding import PartitionSpec as P

inv_temp = 20.0
clip_norm = 256.0


def silu_slope(pre):
    sigma = jax.nn.sigmoid(pre)
    return sigma * (1.0 + pre * (1.0 - sigma))


def contract_rows(left, right):
    return lax.dot_general(
        left, right, (((0,), (0,)), ((), ())), preferred_element_type=jnp.float32
    )


def contract_cols(left, right):
    return lax.dot_general(
        left, right, (((1,), (1,)), ((), ())), preferred_element_type=jnp.float32
    )


def tower_forward(features, first, second, third):
    first_pre = jnp.dot(features, first, preferred_element_type=jnp.float32)
    first_act = jax.nn.silu(first_pre).astype(jnp.bfloat16)
    second_pre = jnp.dot(first_act, second, preferred_element_type=jnp.float32)
    second_act = jax.nn.silu(second_pre).astype(jnp.bfloat16)
    embedding = jnp.dot(second_act, third, preferred_element_type=jnp.float32)
    inv_norm = lax.rsqrt(jnp.sum(embedding * embedding, axis=1, keepdims=True) + 1.0)
    unit = (embedding * inv_norm).astype(jnp.bfloat16)
    return ((first_pre, first_act, second_pre, second_act, embedding, inv_norm), unit)


def tower_backward(features, second, third, saved, unit_grad):
    first_pre, first_act, second_pre, second_act, embedding, inv_norm = saved
    along = jnp.sum(embedding * unit_grad, axis=1, keepdims=True)
    embed_grad = (inv_norm * unit_grad - inv_norm * inv_norm * inv_norm * embedding * along).astype(
        jnp.bfloat16
    )
    third_grad = contract_rows(second_act, embed_grad)
    second_slope = (contract_cols(embed_grad, third) * silu_slope(second_pre)).astype(jnp.bfloat16)
    second_grad = contract_rows(first_act, second_slope)
    first_slope = (contract_cols(second_slope, second) * silu_slope(first_pre)).astype(jnp.bfloat16)
    first_grad = contract_rows(features, first_slope)
    return (first_grad, second_grad, third_grad)


def per_device(
    query_features,
    positive_features,
    negative_features,
    positive_ids,
    positive_counts,
    negative_ids,
    negative_counts,
    query_first,
    query_second,
    query_third,
    item_first,
    item_second,
    item_third,
):
    own_rows = query_features.shape[0]
    query_saved, query_unit = tower_forward(query_features, query_first, query_second, query_third)
    item_features = jnp.concatenate([positive_features, negative_features], axis=0)
    item_saved, item_unit = tower_forward(item_features, item_first, item_second, item_third)
    positive_unit = item_unit[:own_rows]
    negative_unit = item_unit[own_rows:]
    group_unit = lax.all_gather(query_unit, "neg", axis=0, tiled=True)
    shard_unit = lax.all_gather(negative_unit, "dp", axis=0, tiled=True)
    scores = (
        contract_cols(group_unit, shard_unit) * inv_temp
        - jnp.log(negative_counts.astype(jnp.float32))[None, :]
    )
    weights = jnp.where(positive_ids[:, None] != negative_ids[None, :], jnp.exp(scores), 0.0)
    positive_logit = jnp.sum(
        query_unit.astype(jnp.float32) * positive_unit.astype(jnp.float32), axis=1
    ) * inv_temp - jnp.log(positive_counts.astype(jnp.float32))
    positive_exp = jnp.exp(positive_logit)
    offset = lax.axis_index("neg") * own_rows
    partial_value = jnp.sum(weights, axis=1)
    own_part = lax.dynamic_slice(partial_value, (offset,), (own_rows,)) + positive_exp
    partial_value = lax.dynamic_update_slice(partial_value, own_part, (offset,))
    denom = lax.psum(partial_value, "neg")
    own_denom = lax.dynamic_slice(denom, (offset,), (own_rows,))
    loss_part = jnp.sum(jnp.log(own_denom) - positive_logit)
    softmax_weights = (weights / denom[:, None]).astype(jnp.bfloat16)
    positive_slope = positive_exp / own_denom - 1.0
    block = softmax_weights
    query_sum = lax.psum_scatter(
        jnp.dot(block, shard_unit, preferred_element_type=jnp.float32),
        "neg",
        scatter_dimension=0,
        tiled=True,
    )
    query_grad = (
        query_sum + positive_slope[:, None] * positive_unit.astype(jnp.float32)
    ) * inv_temp
    block = softmax_weights
    negative_sum = lax.psum_scatter(
        contract_rows(block, group_unit), "dp", scatter_dimension=0, tiled=True
    )
    positive_grad = positive_slope[:, None] * query_unit.astype(jnp.float32) * inv_temp
    item_grad = jnp.concatenate([positive_grad, negative_sum * inv_temp], axis=0)
    query_grads = tower_backward(query_features, query_second, query_third, query_saved, query_grad)
    item_grads = tower_backward(item_features, item_second, item_third, item_saved, item_grad)
    gradients = query_grads + item_grads
    loss_sum = lax.psum(loss_part, ("dp", "neg"))
    mean_loss = loss_sum / (own_rows * lax.axis_size("dp") * lax.axis_size("neg"))
    vectors = tuple((gradient.reshape(-1) for gradient in gradients))
    pieces = (
        lax.psum_scatter(vectors[0], ("dp", "neg"), scatter_dimension=0, tiled=True),
        lax.psum_scatter(vectors[1], ("dp", "neg"), scatter_dimension=0, tiled=True),
        lax.psum_scatter(vectors[2], ("dp", "neg"), scatter_dimension=0, tiled=True),
        lax.psum_scatter(vectors[3], ("dp", "neg"), scatter_dimension=0, tiled=True),
        lax.psum_scatter(vectors[4], ("dp", "neg"), scatter_dimension=0, tiled=True),
        lax.psum_scatter(vectors[5], ("dp", "neg"), scatter_dimension=0, tiled=True),
    )
    squares = jnp.zeros((), jnp.float32)
    for piece in pieces:
        squares = squares + jnp.sum(piece * piece)
    grad_norm = jnp.sqrt(lax.psum(squares, ("dp", "neg")))
    clip_factor = clip_norm / jnp.maximum(grad_norm, clip_norm)
    scaled = tuple((piece * clip_factor for piece in pieces))
    gathered = (
        lax.all_gather(scaled[0], "neg", axis=0, tiled=True),
        lax.all_gather(scaled[1], "neg", axis=0, tiled=True),
        lax.all_gather(scaled[2], "neg", axis=0, tiled=True),
        lax.all_gather(scaled[3], "neg", axis=0, tiled=True),
        lax.all_gather(scaled[4], "neg", axis=0, tiled=True),
        lax.all_gather(scaled[5], "neg", axis=0, tiled=True),
    )
    clipped = tuple(
        (vector.reshape(-1, gradient.shape[1]) for vector, gradient in zip(gathered, gradients))
    )
    return (mean_loss, clipped[0], clipped[1], clipped[2], clipped[3], clipped[4], clipped[5])


def solution(mesh):
    placed = (
        P(("dp", "neg"), None),
        P(("dp", "neg"), None),
        P(("neg", "dp"), None),
        P("dp"),
        P(("dp", "neg")),
        P("neg"),
        P("neg"),
        P(),
        P(),
        P(),
        P(),
        P(),
        P(),
    )
    return jax.shard_map(
        per_device,
        mesh=mesh,
        in_specs=placed,
        out_specs=(
            P(),
            P("dp", None),
            P("dp", None),
            P("dp", None),
            P("dp", None),
            P("dp", None),
            P("dp", None),
        ),
        check_vma=False,
    )
```

profile of v0, /device:TPU:0, one launch (start us, length us, event | category | flops | bytes accessed | tf_op | source)
XLA Modules:
  0.0 522.5 jit_solution(4157057472190406445)
XLA Ops:
  7.2 1.0 constant_dynamic-update-slice_fusion.1
  8.3 1.1 constant_dynamic-update-slice_fusion
  9.4 2.9 multiply_convert_fusion.1
  12.3 2.3 multiply_convert_fusion.3
  14.6 0.9 copy-done.3
  17.3 2.9 multiply_convert_fusion.6
  21.0 8.6 %all_gather.24 = bf16[1024,256]{0,1:T(8,128)(2,1)S(1)} all-gather(bf16[256,256]{0,1:T(8,128)(2,1)S(1)} %get-tuple-element.16), channel_id=1, replica_groups=mesh['dp'=8,'neg'=4] {'neg'}, dimensions={0}, use_global_device_ids=true | all-gather | bytes 655360 | tf_op jit(solution)/shard_map/all_gather | solution.py:73
  29.6 40.3 %all-gather.2.cloned.1.call-done = bf16[4096,256]{0,1:T(8,128)(2,1)} async-done(((bf16[512,256]{0,1:T(8,128)(2,1)}), bf16[4096,256]{0,1:T(8,128)(2,1)}) %all-gather.2.cloned.1.call-update) | async-done | bytes 2097168 | tf_op jit(solution)/shard_map/all_gather | solution.py:74
  70.0 9.7 %fusion = (f32[1024]{0:T(1024)S(1)}, f32[1024,4096]{1,0:T(8,128)}) fusion(f32[4096]{0:T(1024)S(1)} %convert_log_fusion, s32[4096]{0:T(1024)S(1)} %copy-done.18, s32[1024]{0:T(1024)S(1)} %copy-done.19, bf16[1024,256]{0,1:T(8,128)(2,1)S(1)} %all_gather.24, bf16[4096,256]{0,1:T(8,128)(2,1)} %all-gather.2.cloned.1.call-done), kind=kOutput, calls=%fused_computation.2 | convolution fusion | flops 2168454144 | bytes 19439616 | tf_op jit(solution)/shard_map/dot_general | solution.py:22
  79.8 5.8 %psum.21 = f32[1024]{0:T(1024)S(1)} all-reduce(f32[1024]{0:T(1024)S(1)} %add_dynamic-update-slice_fusion), channel_id=1, replica_groups=mesh['dp'=8,'neg'=4] {'neg'}, use_global_device_ids=true, to_apply=%region_4.5 | all-reduce | flops 1024 | bytes 8192 | tf_op jit(solution)/shard_map/psum | solution.py:88
  85.6 8.4 %divide_convert_fusion = bf16[1024,4096]{1,0:T(8,128)(2,1)S(1)} fusion(f32[1024,4096]{1,0:T(8,128)} %get-tuple-element.37, f32[1024]{0:T(1024)S(1)} %psum.21, f32[4096]{0:T(1024)S(1)} %convert_log_fusion, s32[4096]{0:T(1024)S(1)} %copy-done.18, s32[1024]{0:T(1024)S(1)} %copy-done.19), kind=kLoop, calls=%fused_computation | loop fusion | flops 25165824 | bytes 25206784 | tf_op jit(solution)/shard_map/convert_element_type | solution.py:91
  94.0 3.2 copy-done.2
  97.2 3.3 fusion.15
  100.8 7.7 %fusion.16 = f32[4096,256]{0,1:T(8,128)} fusion(bf16[1024,256]{0,1:T(8,128)(2,1)S(1)} %all_gather.24, bf16[1024,4096]{1,0:T(8,128)(2,1)} %copy-done.2), kind=kOutput, calls=%fused_computation.73 | convolution fusion | flops 2147483648 | bytes 13107200 | tf_op jit(solution)/shard_map/dot_general | solution.py:16
  109.2 14.5 %reduce-scatter.3.cloned.1.call-done = f32[256,256]{0,1:T(8,128)} async-done(((f32[1024,256]{0,1:T(8,128)}), f32[256,256]{0,1:T(8,128)}) %reduce-scatter.3.cloned.1.call-update) | async-done | bytes 262160 | tf_op jit(solution)/shard_map/reduce_scatter | solution.py:94
  123.8 1.0 fusion.8
  124.8 1.1 subtract_convert_fusion.1
  125.9 1.4 fusion.2
  127.3 3.5 convolution_bitcast_fusion.1
  130.8 1.9 copy.26
  132.7 1.8 copy.30
  135.1 1.9 copy.31
  137.2 1.1 copy.32
  138.3 77.8 %reduce-scatter.5.cloned.1.call-done = f32[512,256]{0,1:T(8,128)} async-done(((f32[4096,256]{0,1:T(8,128)}), f32[512,256]{0,1:T(8,128)}) %reduce-scatter.5.cloned.1.call-update) | async-done | bytes 524304 | tf_op jit(solution)/shard_map/reduce_scatter | solution.py:104
  216.1 1.1 broadcast_multiply_fusion
  217.9 1.1 copy.35
  219.8 0.9 copy-done.25
  220.7 1.0 convolution_bitcast_fusion.2
  221.7 1.9 copy.34
  223.6 4.5 convolution_bitcast_fusion.3
  228.1 1.8 copy.33
  229.9 191.2 %all-reduce.10.cloned.1.call-done = (f32[524288]{0:T(1024)}, f32[524288]{0:T(1024)}, f32[131072]{0:T(1024)}, f32[524288]{0:T(1024)}, f32[524288]{0:T(1024)}, /*index=5*/f32[131072]{0:T(1024)}) async-done(((f32[524288]{0:T(1024)}, f32[524288]{0:T(1024)}, f32[131072]{0:T(1024)}, f32[524288]{0:T(1024)}, f32[524288]{0:T(1024)}, /*index=5*/f32[131072]{0:T(1024)}), (f32[524288]{0:T(1024)}, f32[524288]{0:T(1024)}, ...) | async-done | bytes 9437200
  421.1 1.5 multiply_reduce_fusion.4
  422.6 1.5 multiply_reduce_fusion.6
  425.4 1.4 multiply_reduce_fusion.8
  429.4 40.4 %all-reduce.6 = (f32[]{:T(128)}, f32[]{:T(128)}) all-reduce(f32[]{:T(128)} %get-tuple-element.18, f32[]{:T(128)S(6)} %add.128), channel_id=1, replica_groups=mesh['dp'=8,'neg'=4] {'dp','neg'}, use_global_device_ids=true, to_apply=%region_6.7 | all-reduce | flops 2 | bytes 16 | tf_op jit(solution)/shard_map/psum | solution.py:112
  471.3 0.8 dynamic-slice_multiply_fusion
  472.1 0.9 dynamic-slice_multiply_fusion.1
  473.8 0.8 dynamic-slice_multiply_fusion.2
  474.6 0.8 dynamic-slice_multiply_fusion.3
  475.5 5.5 %all_gather.31 = f32[16384]{0:T(1024)S(1)} all-gather(f32[4096]{0:T(1024)S(1)} %dynamic-slice_multiply_fusion.4), channel_id=1, replica_groups=mesh['dp'=8,'neg'=4] {'neg'}, dimensions={0}, use_global_device_ids=true | all-gather | bytes 81920 | tf_op jit(solution)/shard_map/all_gather | solution.py:135
  481.6 6.3 %all_gather.30 = f32[65536]{0:T(1024)S(1)} all-gather(f32[16384]{0:T(1024)S(1)} %dynamic-slice_multiply_fusion), channel_id=1, replica_groups=mesh['dp'=8,'neg'=4] {'neg'}, dimensions={0}, use_global_device_ids=true | all-gather | bytes 327680 | tf_op jit(solution)/shard_map/all_gather | solution.py:134
  488.6 5.8 %all_gather.29 = f32[65536]{0:T(1024)S(1)} all-gather(f32[16384]{0:T(1024)S(1)} %dynamic-slice_multiply_fusion.1), channel_id=1, replica_groups=mesh['dp'=8,'neg'=4] {'neg'}, dimensions={0}, use_global_device_ids=true | all-gather | bytes 327680 | tf_op jit(solution)/shard_map/all_gather | solution.py:133
  494.4 0.7 reshape.90
  495.2 5.2 all_gather.28
  501.0 5.8 %all_gather.27 = f32[65536]{0:T(1024)S(1)} all-gather(f32[16384]{0:T(1024)S(1)} %dynamic-slice_multiply_fusion.2), channel_id=1, replica_groups=mesh['dp'=8,'neg'=4] {'neg'}, dimensions={0}, use_global_device_ids=true | all-gather | bytes 327680 | tf_op jit(solution)/shard_map/all_gather | solution.py:131
  507.6 5.8 %all_gather.26 = f32[65536]{0:T(1024)S(1)} all-gather(f32[16384]{0:T(1024)S(1)} %dynamic-slice_multiply_fusion.3), channel_id=1, replica_groups=mesh['dp'=8,'neg'=4] {'neg'}, dimensions={0}, use_global_device_ids=true | all-gather | bytes 327680 | tf_op jit(solution)/shard_map/all_gather | solution.py:130
  513.5 0.7 reshape.87
  (82 shorter events, 10.2 us)
Async XLA Ops:
  7.2 2.2 copy-start
  7.2 62.8 %all-gather.2.cloned.1.call-start = ((), (), s32[]{:S(2)}) async-start(), calls=%async_computation.2 | async-start | bytes 2359296 | tf_op jit(solution)/shard_map/all_gather | solution.py:74
  9.4 2.9 copy-start.15
  9.4 2.9 copy-start.22
  12.3 2.3 copy-start.23
  12.3 3.2 copy-start.12
  14.6 0.9 copy-start.3
  14.6 2.2 copy-start.7
  14.6 2.2 copy-start.11
  16.7 107.0 %reduce-scatter.3.cloned.1.call-start = ((), (), s32[]{:S(2)}) async-start(), calls=%async_computation.3 | async-start | bytes 1310720 | tf_op jit(solution)/shard_map/reduce_scatter | solution.py:94
  17.2 3.0 copy-start.8
  17.2 3.0 copy-start.14
  17.3 12.3 %copy-start.17 = (s32[4096]{0:T(1024)S(1)}, s32[4096]{0:T(1024)}, u32[]{:S(2)}) copy-start(s32[4096]{0:T(1024)} %param.19) | copy-start | bytes 49156
  17.3 52.7 %copy-start.18 = (s32[4096]{0:T(1024)S(1)}, s32[4096]{0:T(1024)}, u32[]{:S(2)}) copy-start(s32[4096]{0:T(1024)} %param.18) | copy-start | bytes 49156
  17.3 52.7 %copy-start.19 = (s32[1024]{0:T(1024)S(1)}, s32[1024]{0:T(1024)}, u32[]{:S(2)}) copy-start(s32[1024]{0:T(1024)} %param.16) | copy-start | bytes 12292
  20.2 0.7 copy-start.5
  29.6 50.0 %copy-start.20 = (s32[256]{0:T(256)S(1)}, s32[256]{0:T(256)}, u32[]{:S(2)}) copy-start(s32[256]{0:T(256)} %param.17) | copy-start | bytes 3076
  85.6 11.6 %copy-start.21 = (bf16[4096,256]{0,1:T(8,128)(2,1)S(1)}, bf16[4096,256]{0,1:T(8,128)(2,1)}, u32[]{:S(2)}) copy-start(bf16[4096,256]{0,1:T(8,128)(2,1)} %all-gather.2.cloned.1.call-done) | copy-start | bytes 6291460
  94.0 3.2 copy-start.2
  100.6 115.6 %reduce-scatter.5.cloned.1.call-start = ((), (), s32[]{:S(2)}) async-start(), calls=%async_computation.4 | async-start | bytes 4718592 | tf_op jit(solution)/shard_map/reduce_scatter | solution.py:104
  108.5 312.6 %all-reduce.10.cloned.1.call-start = ((), (), s32[]{:S(2)}) async-start(), calls=%async_computation.5 | async-start | bytes 18874368
  124.8 2.5 copy-start.9
  132.7 1.8 copy-start.10
  135.0 1.9 copy-start.6
  138.3 79.2 %copy-start.4 = (bf16[768,512]{1,0:T(8,128)(2,1)S(1)}, bf16[768,512]{1,0:T(8,128)(2,1)}, u32[]{:S(2)}) copy-start(bf16[768,512]{1,0:T(8,128)(2,1)} %copy-done.3) | copy-start | bytes 2359300
  217.3 1.7 copy-start.13
  217.3 1.7 copy-start.26
  219.1 1.6 copy-start.24
  219.8 0.9 copy-start.25
  221.7 1.9 copy-start.16
  472.1 42.7 %copy-start.1 = (bf16[512,1024]{1,0:T(8,128)(2,1)S(1)}, bf16[512,1024]{1,0:T(8,128)(2,1)}, u32[]{:S(2)}) copy-start(bf16[512,1024]{1,0:T(8,128)(2,1)} %param.23) | copy-start | bytes 3145732
Sparse Core Ops, SparseCore 0:
  16.8 53.0 all-gather.1
  100.7 23.0 reduce-scatter.2
  127.4 88.6 reduce-scatter.4
  230.0 191.0 all-reduce.9
where the time goes:
time: 524 us; the launch traced here: 523 us
  waiting for transfers between devices  324 us (62%)
  blocking collectives  89.4 us (17%)
  matrix products  42.1 us (8%)
  local copies, waits for them, and re-layouts  24.1 us (5%)
  other arithmetic  22.1 us (4%)
  between operations  20.5 us (4%)
    unnamed x5, waiting for transfers between devices  191 us
    reduce_scatter x1, waiting for transfers between devices, per_device(): lax.psum_scatter(contract_rows(block, group_unit), 'dp', scatter_dimensio...  77.8 us
    psum x1, blocking collectives, per_device(): loss_sum = lax.psum(loss_part, ('dp', 'neg'))  40.4 us
    all_gather x1, waiting for transfers between devices, per_device(): shard_unit = lax.all_gather(negative_unit, 'dp', axis=0, tiled=True)  40.3 us
    dot_general x7, matrix products, contract_rows(): lax.dot_general(left, right, (((0,), (0,)), ((), ())), preferred_element_...  17.9 us
    unnamed x61, local copies, waits for them, and re-layouts  16.1 us
    reduce_scatter x1, waiting for transfers between devices, per_device(): lax.psum_scatter(jnp.dot(block, shard_unit, preferred_element_type=jnp.fl...  14.5 us
    dot_general x3, matrix products, contract_cols(): lax.dot_general(left, right, (((1,), (1,)), ((), ())), preferred_element_...  11.7 us
  transfers between devices with their start and end apart: 4, of which 4 were waited for; matrix products, arithmetic and copies ran while one was open for 5% of the time, Pallas kernels for 0%

commit v1 on v0

--- a/solution.py
+++ b/solution.py
@@ -1,6 +1,10 @@
+import functools
+
 import jax
 import jax.numpy as jnp
 from jax import lax
+from jax.experimental import pallas as pl
+from jax.experimental.pallas import tpu as pltpu
 from jax.sharding import PartitionSpec as P
 
 inv_temp = 20.0
@@ -47,6 +51,172 @@
     first_slope = (contract_cols(second_slope, second) * silu_slope(first_pre)).astype(jnp.bfloat16)
     first_grad = contract_rows(features, first_slope)
     return (first_grad, second_grad, third_grad)
+
+
+pack_columns = 256
+vmem = pl.BlockSpec(memory_space=pltpu.VMEM)
+
+
+def greet(ndp, nneg, me_dp, me_neg):
+    barrier = pltpu.get_barrier_semaphore()
+    for k in range(1, nneg):
+        pl.semaphore_signal(
+            barrier, inc=1, device_id={"neg": lax.rem(me_neg + k, nneg)}, device_id_type=pl.DeviceIdType.MESH
+        )
+    for k in range(1, ndp):
+        pl.semaphore_signal(
+            barrier, inc=1, device_id={"dp": lax.rem(me_dp + k, ndp)}, device_id_type=pl.DeviceIdType.MESH
+        )
+    pl.semaphore_wait(barrier, (nneg - 1) + (ndp - 1))
+
+
+def send(src, dst, send_sem, recv_sem, axis, target):
+    copy = pltpu.make_async_remote_copy(
+        src_ref=src,
+        dst_ref=dst,
+        send_sem=send_sem,
+        recv_sem=recv_sem,
+        device_id={axis: target},
+        device_id_type=pl.DeviceIdType.MESH,
+    )
+    copy.start()
+    return copy
+
+
+def share(axis, n, me, src_of, dst, send_sem, recv_sem):
+    return [
+        send(src_of(lax.rem(me + k, n)), dst.at[me], send_sem.at[k], recv_sem.at[k], axis, lax.rem(me + k, n))
+        for k in range(1, n)
+    ]
+
+
+def finish(copies):
+    for copy in copies:
+        copy.wait()
+
+
+def gather_kernel(ndp, nneg, query_ref, negative_ref, group_ref, shard_ref, qs, qr, ns, nr):
+    me_dp, me_neg = lax.axis_index("dp"), lax.axis_index("neg")
+    greet(ndp, nneg, me_dp, me_neg)
+    copies = share("dp", ndp, me_dp, lambda t: negative_ref, shard_ref, ns, nr)
+    copies += share("neg", nneg, me_neg, lambda t: query_ref, group_ref, qs, qr)
+    group_ref[me_neg] = query_ref[...]
+    shard_ref[me_dp] = negative_ref[...]
+    finish(copies)
+
+
+def query_kernel(ndp, nneg, part_ref, denom_ref, sum_ref, total_ref, land, denom_land, qs, qr, ds, dr):
+    me_dp, me_neg = lax.axis_index("dp"), lax.axis_index("neg")
+    greet(1, nneg, me_dp, me_neg)
+    small = share("neg", nneg, me_neg, lambda t: denom_ref, denom_land, ds, dr)
+    copies = share("neg", nneg, me_neg, lambda t: part_ref.at[t], land, qs, qr)
+    total = denom_ref[...]
+    finish(small)
+    for k in range(1, nneg):
+        total = total + denom_land[lax.rem(me_neg + k, nneg)]
+    total_ref[...] = total
+    finish(copies)
+    result = part_ref[me_neg].astype(jnp.float32)
+    for k in range(1, nneg):
+        result = result + land[lax.rem(me_neg + k, nneg)].astype(jnp.float32)
+    sum_ref[...] = result
+
+
+def negative_kernel(ndp, nneg, part_ref, sum_ref, land, ns, nr):
+    me_dp, me_neg = lax.axis_index("dp"), lax.axis_index("neg")
+    greet(ndp, 1, me_dp, me_neg)
+    copies = share("dp", ndp, me_dp, lambda t: part_ref.at[t], land, ns, nr)
+    finish(copies)
+    result = part_ref[me_dp].astype(jnp.float32)
+    for k in range(1, ndp):
+        result = result + land[lax.rem(me_dp + k, ndp)].astype(jnp.float32)
+    sum_ref[...] = result
+
+
+def weight_kernel(
+    ndp, nneg, packed_ref, loss_ref, gathered_ref, stats_ref,
+    core_land, core_sum, row_land, row_sum, dp_land, stat_dp, stat_dp_land, stat_neg, stat_neg_land,
+    cs, cr, xs, xr, ps, pr, ss, sr, ts, tr, gs, gr,
+):
+    me_dp, me_neg = lax.axis_index("dp"), lax.axis_index("neg")
+    nx = nneg // 2
+    me_x, me_core = me_neg // 2, lax.rem(me_neg, 2)
+    other = 1 - me_core
+    greet(ndp, nneg, me_dp, me_neg)
+    core = [
+        send(packed_ref.at[2 * x + other], core_land.at[x], cs.at[x], cr.at[x], "neg", 2 * me_x + other)
+        for x in range(nx)
+    ]
+    row = []
+    for k in list(range(1, nx)) + [0]:
+        x = lax.rem(me_x + k, nx)
+        if k == 1 or nx == 1:
+            finish(core)
+
+        def core_add(d, carry):
+            core_sum[x, d] = (
+                packed_ref[2 * x + me_core, d].astype(jnp.float32) + core_land[x, d].astype(jnp.float32)
+            ).astype(jnp.bfloat16)
+            return carry
+
+        lax.fori_loop(0, ndp, core_add, 0)
+        if k:
+            row.append(
+                send(core_sum.at[x], row_land.at[k], xs.at[k], xr.at[k], "neg", 2 * x + me_core)
+            )
+    finish(row)
+
+    def row_add(d, carry):
+        value = core_sum[me_x, d].astype(jnp.float32)
+        for k in range(1, nx):
+            value = value + row_land[k, d].astype(jnp.float32)
+        row_sum[d] = value.astype(jnp.bfloat16)
+        return carry
+
+    lax.fori_loop(0, ndp, row_add, 0)
+    finish(share("dp", ndp, me_dp, lambda t: row_sum.at[t], dp_land, ps, pr))
+    piece = row_sum[me_dp].astype(jnp.float32)
+    for k in range(1, ndp):
+        piece = piece + dp_land[lax.rem(me_dp + k, ndp)].astype(jnp.float32)
+    gathered_ref[me_neg] = piece.astype(jnp.bfloat16)
+    lane = lax.broadcasted_iota(jnp.int32, (8, 128), 1)
+    stat_dp[...] = jnp.where(lane == 0, jnp.sum(piece * piece), loss_ref[0])
+    stat_copies = share("dp", ndp, me_dp, lambda t: stat_dp, stat_dp_land, ss, sr)
+    gather = share("neg", nneg, me_neg, lambda t: gathered_ref.at[me_neg], gathered_ref, gs, gr)
+    finish(stat_copies)
+    total = stat_dp[...]
+    for k in range(1, ndp):
+        total = total + stat_dp_land[lax.rem(me_dp + k, ndp)]
+    stat_neg[...] = total
+    finish(share("neg", nneg, me_neg, lambda t: stat_neg, stat_neg_land, ts, tr))
+    total = stat_neg[...]
+    for k in range(1, nneg):
+        total = total + stat_neg_land[lax.rem(me_neg + k, nneg)]
+    stats_ref[...] = total
+    finish(gather)
+
+
+def call(kernel, collective, ndp, nneg, out_shape, scratch, in_specs):
+    return pl.pallas_call(
+        functools.partial(kernel, ndp, nneg),
+        out_shape=out_shape,
+        in_specs=in_specs,
+        out_specs=tuple(vmem for _ in out_shape),
+        scratch_shapes=scratch,
+        compiler_params=pltpu.CompilerParams(
+            collective_id=collective, has_side_effects=True, vmem_limit_bytes=48 * 1024 * 1024
+        ),
+    )
+
+
+def sems(*counts):
+    return [pltpu.SemaphoreType.DMA((count,)) for count in counts]
+
+
+def to_packed(gradient, ndp):
+    rows, columns = gradient.shape
+    blocks = gradient.astype(jnp.bfloat16).reshape(ndp, rows // ndp, columns)
+    return [blocks[:, :, c : c + pack_columns] for c in range(0, columns, pack_columns)]
 
 
 def per_device(
@@ -70,8 +240,22 @@
     item_saved, item_unit = tower_forward(item_features, item_first, item_second, item_third)
     positive_unit = item_unit[:own_rows]
     negative_unit = item_unit[own_rows:]
-    group_unit = lax.all_gather(query_unit, "neg", axis=0, tiled=True)
-    shard_unit = lax.all_gather(negative_unit, "dp", axis=0, tiled=True)
+    ndp, nneg = lax.axis_size("dp"), lax.axis_size("neg")
+    width = query_unit.shape[1]
+    group_unit, shard_unit = call(
+        gather_kernel,
+        0,
+        ndp,
+        nneg,
+        (
+            jax.ShapeDtypeStruct((nneg,) + query_unit.shape, jnp.bfloat16),
+            jax.ShapeDtypeStruct((ndp,) + negative_unit.shape, jnp.bfloat16),
+        ),
+        sems(nneg, nneg, ndp, ndp),
+        [vmem, vmem],
+    )(query_unit, negative_unit)
+    group_unit = group_unit.reshape(-1, width)
+    shard_unit = shard_unit.reshape(-1, width)
     scores = (
         contract_cols(group_unit, shard_unit) * inv_temp
         - jnp.log(negative_counts.astype(jnp.float32))[None, :]
@@ -85,59 +269,90 @@
     partial_value = jnp.sum(weights, axis=1)
     own_part = lax.dynamic_slice(partial_value, (offset,), (own_rows,)) + positive_exp
     partial_value = lax.dynamic_update_slice(partial_value, own_part, (offset,))
-    denom = lax.psum(partial_value, "neg")
+    block = weights.astype(jnp.bfloat16)
+    query_part = jnp.dot(block, shard_unit, preferred_element_type=jnp.float32).astype(jnp.bfloat16)
+    denom_shape = (nneg * own_rows // 128, 128)
+    query_total, denom = call(
+        query_kernel,
+        1,
+        ndp,
+        nneg,
+        (
+            jax.ShapeDtypeStruct((own_rows, width), jnp.float32),
+            jax.ShapeDtypeStruct(denom_shape, jnp.float32),
+        ),
+        [
+            pltpu.VMEM((nneg, own_rows, width), jnp.bfloat16),
+            pltpu.VMEM((nneg,) + denom_shape, jnp.float32),
+        ]
+        + sems(nneg, nneg, nneg, nneg),
+        [vmem, vmem],
+    )(query_part.reshape(nneg, own_rows, width), partial_value.reshape(denom_shape))
+    denom = denom.reshape(-1)
     own_denom = lax.dynamic_slice(denom, (offset,), (own_rows,))
     loss_part = jnp.sum(jnp.log(own_denom) - positive_logit)
-    softmax_weights = (weights / denom[:, None]).astype(jnp.bfloat16)
     positive_slope = positive_exp / own_denom - 1.0
-    block = softmax_weights
-    query_sum = lax.psum_scatter(
-        jnp.dot(block, shard_unit, preferred_element_type=jnp.float32),
-        "neg",
-        scatter_dimension=0,
-        tiled=True,
-    )
+    query_sum = query_total / own_denom[:, None]
+    scaled_unit = (group_unit.astype(jnp.float32) / denom[:, None]).astype(jnp.bfloat16)
+    negative_part = contract_rows(block, scaled_unit).astype(jnp.bfloat16)
+    negative_rows = negative_unit.shape[0]
+    (negative_sum,) = call(
+        negative_kernel,
+        2,
+        ndp,
+        nneg,
+        (jax.ShapeDtypeStruct((negative_rows, width), jnp.float32),),
+        [pltpu.VMEM((ndp, negative_rows, width), jnp.bfloat16)] + sems(ndp, ndp),
+        [vmem],
+    )(negative_part.reshape(ndp, negative_rows, width))
     query_grad = (
         query_sum + positive_slope[:, None] * positive_unit.astype(jnp.float32)
     ) * inv_temp
-    block = softmax_weights
-    negative_sum = lax.psum_scatter(
-        contract_rows(block, group_unit), "dp", scatter_dimension=0, tiled=True
-    )
     positive_grad = positive_slope[:, None] * query_unit.astype(jnp.float32) * inv_temp
     item_grad = jnp.concatenate([positive_grad, negative_sum * inv_temp], axis=0)
     query_grads = tower_backward(query_features, query_second, query_third, query_saved, query_grad)
     item_grads = tower_backward(item_features, item_second, item_third, item_saved, item_grad)
     gradients = query_grads + item_grads
-    loss_sum = lax.psum(loss_part, ("dp", "neg"))
-    mean_loss = loss_sum / (own_rows * lax.axis_size("dp") * lax.axis_size("neg"))
-    vectors = tuple((gradient.reshape(-1) for gradient in gradients))
-    pieces = (
-        lax.psum_scatter(vectors[0], ("dp", "neg"), scatter_dimension=0, tiled=True),
-        lax.psum_scatter(vectors[1], ("dp", "neg"), scatter_dimension=0, tiled=True),
-        lax.psum_scatter(vectors[2], ("dp", "neg"), scatter_dimension=0, tiled=True),
-        lax.psum_scatter(vectors[3], ("dp", "neg"), scatter_dimension=0, tiled=True),
-        lax.psum_scatter(vectors[4], ("dp", "neg"), scatter_dimension=0, tiled=True),
-        lax.psum_scatter(vectors[5], ("dp", "neg"), scatter_dimension=0, tiled=True),
-    )
-    squares = jnp.zeros((), jnp.float32)
-    for piece in pieces:
-        squares = squares + jnp.sum(piece * piece)
-    grad_norm = jnp.sqrt(lax.psum(squares, ("dp", "neg")))
+    parts = [part for gradient in gradients for part in to_packed(gradient, ndp)]
+    packed = jnp.concatenate(parts, axis=1)
+    rows = packed.shape[1] // nneg
+    packed = packed.reshape(ndp, nneg, rows, pack_columns).transpose(1, 0, 2, 3)
+    nx = nneg // 2
+    piece = (rows, pack_columns)
+    bf16, f32 = jnp.bfloat16, jnp.float32
+    gathered, stats = call(
+        weight_kernel,
+        3,
+        ndp,
+        nneg,
+        (jax.ShapeDtypeStruct((nneg,) + piece, bf16), jax.ShapeDtypeStruct((8, 128), f32)),
+        [
+            pltpu.VMEM((nx, ndp) + piece, bf16),
+            pltpu.VMEM((nx, ndp) + piece, bf16),
+            pltpu.VMEM((nx, ndp) + piece, bf16),
+            pltpu.VMEM((ndp,) + piece, bf16),
+            pltpu.VMEM((ndp,) + piece, bf16),
+            pltpu.VMEM((8, 128), f32),
+            pltpu.VMEM((ndp, 8, 128), f32),
+            pltpu.VMEM((8, 128), f32),
+            pltpu.VMEM((nneg, 8, 128), f32),
+        ]
+        + sems(nx, nx, nx, nx, ndp, ndp, ndp, ndp, nneg, nneg, nneg, nneg),
+        [vmem, pl.BlockSpec(memory_space=pltpu.SMEM)],
+    )(packed, loss_part.reshape(1))
+    grad_norm = jnp.sqrt(stats[0, 0])
+    mean_loss = stats[0, 1] / (own_rows * ndp * nneg)
     clip_factor = clip_norm / jnp.maximum(grad_norm, clip_norm)
-    scaled = tuple((piece * clip_factor for piece in pieces))
-    gathered = (
-        lax.all_gather(scaled[0], "neg", axis=0, tiled=True),
-        lax.all_gather(scaled[1], "neg", axis=0, tiled=True),
-        lax.all_gather(scaled[2], "neg", axis=0, tiled=True),
-        lax.all_gather(scaled[3], "neg", axis=0, tiled=True),
-        lax.all_gather(scaled[4], "neg", axis=0, tiled=True),
-        lax.all_gather(scaled[5], "neg", axis=0, tiled=True),
-    )
-    clipped = tuple(
-        (vector.reshape(-1, gradient.shape[1]) for vector, gradient in zip(gathered, gradients))
-    )
-    return (mean_loss, clipped[0], clipped[1], clipped[2], clipped[3], clipped[4], clipped[5])
+    flat = gathered.reshape(nneg * rows, pack_columns)
+    clipped = []
+    start = 0
+    for gradient in gradients:
+        height, columns = gradient.shape[0] // ndp, gradient.shape[1]
+        groups = columns // pack_columns
+        blocks = [flat[start + g * height : start + (g + 1) * height] for g in range(groups)]
+        start += groups * height
+        clipped.append(jnp.concatenate(blocks, axis=1).astype(jnp.float32) * clip_factor)
+    return (mean_loss, *clipped)
 
 
 def solution(mesh):

time: 524 us -> 236 us (0.45)
  waiting for transfers between devices: 324 us -> 0 us
  Pallas kernels: 0 us -> 182 us
  blocking collectives: 89.4 us -> 0 us
  local copies, waits for them, and re-layouts: 24.1 us -> 7.11 us
  other arithmetic: 22.1 us -> 5.31 us
  between operations: 20.5 us -> 3.77 us
  matrix products: 42.1 us -> 36.7 us
    unnamed x5 -> x0, waiting for transfers between devices: 191 us -> none
    pallas_call x0 -> x4, Pallas kernels: none -> 182 us  [the longest x1 83.8 us: per_device(): call(weight_kernel, 3, ndp, nneg, (jax.ShapeDtypeStruct((nneg,) + piece,...]
    reduce_scatter x2 -> x0, waiting for transfers between devices: 92.4 us -> none  [the longest x1 77.8 us: per_device(): lax.psum_scatter(contract_rows(block, group_unit), 'dp', scatter_dimensio...]
    psum x2 -> x0, blocking collectives: 46.3 us -> none  [the longest x1 40.4 us: per_device(): loss_sum = lax.psum(loss_part, ('dp', 'neg'))]
    all_gather x7 -> x0, blocking collectives: 43.1 us -> none  [the longest x1 8.64 us: per_device(): group_unit = lax.all_gather(query_unit, 'neg', axis=0, tiled=True)]
    all_gather x1 -> x0, waiting for transfers between devices: 40.3 us -> none  [per_device(): shard_unit = lax.all_gather(negative_unit, 'dp', axis=0, tiled=True)]
    unnamed x61 -> x82, local copies, waits for them, and re-layouts: 16.1 us -> 4.57 us
    convert_element_type x1 -> x0, other arithmetic: 8.36 us -> none  [per_device(): softmax_weights = (weights / denom[:, None]).astype(jnp.bfloat16)]
  transfers between devices with their start and end apart: 4 -> 0, of which waited for: 4 -> 0; matrix products, arithmetic and copies ran while one was open for 5% -> 0% of each run, Pallas kernels for 0% -> 0%
where the time goes in v1:
time: 236 us; the launch traced here: 235 us
  Pallas kernels  182 us (77%)
  matrix products  36.7 us (16%)
  local copies, waits for them, and re-layouts  7.11 us (3%)
  other arithmetic  5.31 us (2%)
  between operations  3.77 us (2%)
    pallas_call x1, Pallas kernels, per_device(): call(weight_kernel, 3, ndp, nneg, (jax.ShapeDtypeStruct((nneg,) + piece,...  83.8 us
    pallas_call x1, Pallas kernels, per_device(): call(negative_kernel, 2, ndp, nneg, (jax.ShapeDtypeStruct((negative_rows,...  50.6 us
    pallas_call x1, Pallas kernels, per_device(): call(gather_kernel, 0, ndp, nneg, (jax.ShapeDtypeStruct((nneg,) + query_u...  40 us
    dot_general x7, matrix products, contract_rows(): lax.dot_general(left, right, (((0,), (0,)), ((), ())), preferred_element_...  17.6 us
    pallas_call x1, Pallas kernels, per_device(): call(query_kernel, 1, ndp, nneg, (jax.ShapeDtypeStruct((own_rows, width),...  8.03 us
    dot_general x3, matrix products, contract_cols(): lax.dot_general(left, right, (((1,), (1,)), ((), ())), preferred_element_...  7.75 us
    dot_general x2, matrix products, tower_forward(): first_pre = jnp.dot(features, first, preferred_element_type=jnp.float32)  4.79 us

profile of v1, /device:TPU:0, one launch (start us, length us, event | category | flops | bytes accessed | tf_op | source)
XLA Modules:
  0.0 235.3 jit_solution(16338080419300592721)
XLA Ops:
  0.6 0.0 copy-start
  0.6 1.1 constant_dynamic-update-slice_fusion.1
  1.7 1.1 constant_dynamic-update-slice_fusion
  2.8 2.9 %multiply_convert_fusion.1 = (bf16[768,1024]{1,0:T(8,128)(2,1)S(1)}, f32[768,1024]{1,0:T(8,128)}) fusion(bf16[768,512]{1,0:T(8,128)(2,1)S(1)} %constant_dynamic-update-slice_fusion, bf16[512,1024]{1,0:T(8,128)(2,1)S(1)} %copy-done), kind=kOutput, calls=%fused_computation.6 | convolution fusion | flops 809238528 | bytes 6553600 | tf_op jit(solution)/shard_map/dot_general | solution.py:32
  5.7 2.3 multiply_convert_fusion.3
  8.0 0.4 multiply_reduce_fusion.1
  8.4 0.5 copy-done.8
  8.9 0.3 copy.27
  9.2 0.2 multiply_convert_fusion.5
  9.4 1.9 fusion.19
  11.3 0.0 copy-start.26
  11.4 1.3 multiply_convert_fusion.6
  12.6 0.3 multiply_reduce_fusion.3
  12.9 0.4 copy-done.6
  13.3 0.1 copy.26
  13.5 0.6 broadcast_multiply_fusion.1
  14.1 0.2 fusion.11
  14.3 40.0 %shard_map.180 = (bf16[4,256,256]{2,1,0:T(8,128)(2,1)S(1)}, bf16[8,512,256]{2,1,0:T(8,128)(2,1)S(1)}) custom-call(bf16[256,256]{1,0:T(8,128)(2,1)S(1)} %get-tuple-element.22.query_ref, bf16[512,256]{1,0:T(8,128)(2,1)S(1)} %slice.120.negative_ref), custom_call_target="tpu_custom_call" | custom-call | tf_op jit(solution)/shard_map/pallas_call | solution.py:245
  54.3 5.1 %fusion = (f32[1024]{0:T(1024)S(1)}, bf16[1024,4096]{1,0:T(8,128)(2,1)S(1)}) fusion(f32[4096]{0:T(1024)S(1)} %convert_log_fusion, s32[4096]{0:T(1024)S(1)} %copy-done.26, s32[1024]{0:T(1024)S(1)} %copy-done.27, bf16[1024,256]{1,0:T(8,128)(2,1)S(1)} %bitcast.66, bf16[4096,256]{1,0:T(8,128)(2,1)S(1)} %bitcast.64), kind=kOutput, calls=%fused_computation.1 | convolution fusion | flops 2172648448 | bytes 11051008 | tf_op jit(solution)/shard_map/dot_general | solution.py:26
  59.4 2.3 convolution_convert_fusion.5
  61.8 0.9 copy-done.28
  62.7 0.2 add_dynamic-update-slice_fusion
  62.9 8.0 %shard_map.181 = (f32[256,256]{1,0:T(8,128)S(1)}, f32[8,128]{1,0:T(8,128)S(1)}) custom-call(bf16[4,256,256]{2,1,0:T(8,128)(2,1)S(1)} %bitcast.60, f32[8,128]{1,0:T(8,128)S(1)} %bitcast.61), custom_call_target="tpu_custom_call" | custom-call | tf_op jit(solution)/shard_map/pallas_call | solution.py:275
  71.0 5.9 %convolution_convert_fusion = bf16[4096,256]{1,0:T(8,128)(2,1)S(1)} fusion(bf16[1024,4096]{1,0:T(8,128)(2,1)} %copy-done.28, bf16[1024,256]{1,0:T(8,128)(2,1)S(1)} %bitcast.67, f32[1024]{0:T(1024)S(1)} %bitcast.62), kind=kOutput, calls=%fused_computation.3 | convolution fusion | flops 2149318656 | bytes 11014144 | tf_op jit(solution)/shard_map/dot_general | solution.py:20
  76.9 50.6 %shard_map.182 = f32[512,256]{1,0:T(8,128)S(1)} custom-call(bf16[8,512,256]{2,1,0:T(8,128)(2,1)S(1)} %bitcast.56), custom_call_target="tpu_custom_call" | custom-call | tf_op jit(solution)/shard_map/pallas_call | solution.py:299
  127.6 0.7 subtract_reduce_fusion
  128.3 0.2 fusion.10
  128.6 0.2 multiply_reduce_fusion
  128.8 0.4 subtract_convert_fusion
  129.2 1.6 multiply_convert_fusion.2
  130.8 5.8 %convolution_convert_fusion.2 = bf16[512,1024]{1,0:T(8,128)(2,1)} fusion(bf16[768,512]{1,0:T(8,128)(2,1)} %copy-done.18, f32[768,1024]{1,0:T(8,128)} %get-tuple-element.51, bf16[768,512]{1,0:T(8,128)(2,1)} %multiply_convert_fusion.2, bf16[1024,512]{1,0:T(8,128)(2,1)} %param.24), kind=kOutput, calls=%fused_computation.12 | convolution fusion | flops 1618214912 | bytes 6815744 | tf_op jit(solution)/shard_map/dot_general | solution.py:20
  136.6 0.2 subtract_convert_fusion.1
  136.9 1.0 fusion.3
  137.9 2.6 %convolution_convert_fusion.4 = bf16[1024,512]{0,1:T(8,128)(2,1)S(1)} fusion(bf16[256,512]{1,0:T(8,128)(2,1)S(1)} %copy-done.15, bf16[256,512]{1,0:T(8,128)(2,1)} %fusion.3, bf16[1024,512]{1,0:T(8,128)(2,1)} %param.21, f32[256,1024]{1,0:T(8,128)} %copy-done.3), kind=kOutput, calls=%fused_computation.14 | convolution fusion | flops 539754496 | bytes 3670016 | tf_op jit(solution)/shard_map/dot_general | solution.py:20
  140.7 1.6 convolution_convert_fusion.3
  142.4 0.3 convolution_convert_fusion.7
  142.9 0.8 copy-done.30
  143.7 0.2 copy-done.32
  143.9 1.0 convolution_convert_fusion.1
  145.0 0.0 copy-done.9
  145.1 0.1 copy-done.11
  145.2 0.4 convolution_convert_fusion.6
  145.6 0.3 copy.34
  146.0 83.8 %shard_map.183 = (bf16[4,288,256]{2,1,0:T(8,128)(2,1)S(1)}, f32[8,128]{1,0:T(8,128)S(1)}) custom-call(bf16[4,8,288,256]{3,2,1,0:T(8,128)(2,1)S(1)} %bitcast.55, f32[1]{0:T(128)} %bitcast.16.loss_ref), custom_call_target="tpu_custom_call" | custom-call | tf_op jit(solution)/shard_map/pallas_call | solution.py:323
  229.7 0.7 fusion.18
  231.1 0.7 convert_multiply_fusion.7
  231.8 0.9 convert_multiply_fusion.3
  232.7 0.8 convert_multiply_fusion.4
  (80 shorter events, 0.7 us)
Async XLA Ops:
  0.6 2.2 copy-start
  2.8 5.2 %copy-start.18 = (bf16[768,512]{1,0:T(8,128)(2,1)}, bf16[768,512]{1,0:T(8,128)(2,1)S(1)}, u32[]{:S(2)}) copy-start(bf16[768,512]{1,0:T(8,128)(2,1)S(1)} %constant_dynamic-update-slice_fusion) | copy-start | bytes 2359300
  2.8 2.9 %copy-start.24 = (bf16[1024,512]{1,0:T(8,128)(2,1)S(1)}, bf16[1024,512]{1,0:T(8,128)(2,1)}, u32[]{:S(2)}) copy-start(bf16[1024,512]{1,0:T(8,128)(2,1)} %param.24) | copy-start | bytes 3145732
  5.7 2.3 copy-start.29
  5.7 2.3 copy-start.12
  8.0 0.9 copy-start.8
  8.0 1.4 copy-start.14
  9.2 2.1 copy-start.25
  9.4 4.9 %copy-start.1 = (bf16[768,256]{1,0:T(8,128)(2,1)}, bf16[768,256]{1,0:T(8,128)(2,1)S(1)}, u32[]{:S(2)}) copy-start(bf16[768,256]{1,0:T(8,128)(2,1)S(1)} %multiply_convert_fusion.5) | copy-start | bytes 1179652
  11.3 1.3 copy-start.3
  11.3 1.3 copy-start.16
  11.3 43.0 %copy-start.19 = (s32[4096]{0:T(1024)S(1)}, s32[4096]{0:T(1024)}, u32[]{:S(2)}) copy-start(s32[4096]{0:T(1024)} %param.19) | copy-start | bytes 49156
  11.3 43.0 %copy-start.26 = (s32[4096]{0:T(1024)S(1)}, s32[4096]{0:T(1024)}, u32[]{:S(2)}) copy-start(s32[4096]{0:T(1024)} %param.18) | copy-start | bytes 49156
  11.4 43.0 %copy-start.27 = (s32[1024]{0:T(1024)S(1)}, s32[1024]{0:T(1024)}, u32[]{:S(2)}) copy-start(s32[1024]{0:T(1024)} %param.16) | copy-start | bytes 12292
  12.6 0.7 copy-start.6
  59.4 3.3 %copy-start.28 = (bf16[1024,4096]{1,0:T(8,128)(2,1)}, bf16[1024,4096]{1,0:T(8,128)(2,1)S(1)}, u32[]{:S(2)}) copy-start(bf16[1024,4096]{1,0:T(8,128)(2,1)S(1)} %get-tuple-element.24) | copy-start | bytes 25165828
  59.4 3.3 %copy-start.20 = (s32[256]{0:T(256)S(1)}, s32[256]{0:T(256)}, u32[]{:S(2)}) copy-start(s32[256]{0:T(256)} %param.17) | copy-start | bytes 3076
  76.9 50.7 %copy-start.21 = (s32[256]{0:T(256)S(1)}, s32[256]{0:T(256)}, u32[]{:S(2)}) copy-start(s32[256]{0:T(256)} %param.17) | copy-start | bytes 3076
  76.9 51.4 %copy-start.2 = (bf16[768,256]{1,0:T(8,128)(2,1)S(1)}, bf16[768,256]{1,0:T(8,128)(2,1)}, u32[]{:S(2)}) copy-start(bf16[768,256]{1,0:T(8,128)(2,1)} %copy-done.1) | copy-start | bytes 1179652
  127.5 1.6 copy-start.13
  127.6 1.6 copy-start.33
  129.1 1.7 copy-start.10
  130.8 5.8 %copy-start.22 = (f32[256]{0:T(256)S(1)}, f32[256]{0:T(256)}, u32[]{:S(2)}) copy-start(f32[256]{0:T(256)} %get-tuple-element.45) | copy-start | bytes 3076
  130.8 5.8 %copy-start.23 = (f32[256]{0:T(256)S(1)}, f32[256]{0:T(256)}, u32[]{:S(2)}) copy-start(f32[256]{0:T(256)} %get-tuple-element.46) | copy-start | bytes 3076
  130.8 6.1 %copy-start.17 = (bf16[512,256]{1,0:T(8,128)(2,1)S(1)}, bf16[512,256]{1,0:T(8,128)(2,1)}, u32[]{:S(2)}) copy-start(bf16[512,256]{1,0:T(8,128)(2,1)} %param.22) | copy-start | bytes 786436
  130.8 6.1 %copy-start.31 = (f32[256,512]{1,0:T(8,128)S(1)}, f32[256,512]{1,0:T(8,128)}, u32[]{:S(2)}) copy-start(f32[256,512]{1,0:T(8,128)} %get-tuple-element.49) | copy-start | bytes 1572868
  136.6 1.3 copy-start.15
  137.9 2.8 %copy-start.4 = (f32[256,1024]{1,0:T(8,128)S(1)}, f32[256,1024]{1,0:T(8,128)}, u32[]{:S(2)}) copy-start(f32[256,1024]{1,0:T(8,128)} %copy-done.3) | copy-start | bytes 3145732
  140.7 1.7 copy-start.7
  140.7 2.0 copy-start.5
  142.3 1.4 copy-start.30
  142.3 1.6 copy-start.32
  143.9 1.1 copy-start.9
  143.9 1.2 copy-start.11

commit v2 on v1

--- a/solution.py
+++ b/solution.py
@@ -95,13 +95,85 @@
         copy.wait()
 
 
-def gather_kernel(ndp, nneg, query_ref, negative_ref, group_ref, shard_ref, qs, qr, ns, nr):
+def link(src, dst, sems, index, axis, target):
+    send_sems, recv_sems = sems
+    return pltpu.make_async_remote_copy(
+        src_ref=src,
+        dst_ref=dst,
+        send_sem=send_sems.at[index],
+        recv_sem=recv_sems.at[index],
+        device_id={axis: target},
+        device_id_type=pl.DeviceIdType.MESH,
+    )
+
+
+def gather_kernel(
+    ndp, nneg, query_ref, negative_ref, group_ref, shard_ref, qs, qr, rs, rr, ls, lr, ys, yr
+):
     me_dp, me_neg = lax.axis_index("dp"), lax.axis_index("neg")
+    line = ndp // 2
+    place = me_dp // 2
+    partner = me_dp + 1 - 2 * lax.rem(me_dp, 2)
+    cuts = negative_ref.shape[0]
     greet(ndp, nneg, me_dp, me_neg)
-    copies = share("dp", ndp, me_dp, lambda t: negative_ref, shard_ref, ns, nr)
-    copies += share("neg", nneg, me_neg, lambda t: query_ref, group_ref, qs, qr)
+    goes_right, goes_left = place < line - 1, place > 0
+
+    def block(slot, j, distance):
+        return negative_ref.at[j] if distance == 0 else shard_ref.at[slot, j]
+
+    def right(distance, j):
+        slot = me_dp - 2 * distance
+        return link(block(slot, j, distance), shard_ref.at[slot, j], (rs, rr), (distance + 1) * cuts + j, "dp", lax.rem(me_dp + 2, ndp))
+
+    def left(distance, j):
+        slot = me_dp + 2 * distance
+        return link(block(slot, j, distance), shard_ref.at[slot, j], (ls, lr), (distance + 1) * cuts + j, "dp", lax.rem(me_dp + ndp - 2, ndp))
+
+    def across(offset, j):
+        slot = me_dp + 2 * offset
+        return link(block(slot, j, abs(offset)), shard_ref.at[slot, j], (ys, yr), (offset + line - 1) * cuts + j, "dp", partner)
+
+    def arrival(slot, j, sems, index):
+        return link(shard_ref.at[slot, j], shard_ref.at[slot, j], sems, index, "dp", partner)
+
+    for j in range(cuts):
+        pl.when(goes_right)(lambda j=j: right(0, j).start())
+        pl.when(goes_left)(lambda j=j: left(0, j).start())
+        across(0, j).start()
+    copies = share("neg", nneg, me_neg, lambda t: query_ref, group_ref, qs, qr)
     group_ref[me_neg] = query_ref[...]
     shard_ref[me_dp] = negative_ref[...]
+    for distance in range(1, line):
+        for j in range(cuts):
+
+            @pl.when(place >= distance)
+            def _():
+                arrival(me_dp - 2 * distance, j, (rs, rr), distance * cuts + j).wait_recv()
+                across(-distance, j).start()
+                pl.when(goes_right)(lambda: right(distance, j).start())
+
+            @pl.when(place + distance < line)
+            def _():
+                arrival(me_dp + 2 * distance, j, (ls, lr), distance * cuts + j).wait_recv()
+                across(distance, j).start()
+                pl.when(goes_left)(lambda: left(distance, j).start())
+
+    for distance in range(line):
+        for j in range(cuts):
+
+            @pl.when(place >= distance)
+            def _():
+                across(-distance, j).wait_send()
+                arrival(partner - 2 * distance, j, (ys, yr), (line - 1 - distance) * cuts + j).wait_recv()
+                pl.when(goes_right)(lambda: right(distance, j).wait_send())
+
+            @pl.when(place + distance < line)
+            def _():
+                if distance:
+                    across(distance, j).wait_send()
+                    arrival(partner + 2 * distance, j, (ys, yr), (line - 1 + distance) * cuts + j).wait_recv()
+                pl.when(goes_left)(lambda: left(distance, j).wait_send())
+
     finish(copies)
 
 
@@ -122,78 +194,198 @@
     sum_ref[...] = result
 
 
-def negative_kernel(ndp, nneg, part_ref, sum_ref, land, ns, nr):
+def negative_kernel(
+    ndp, nneg, part_ref, sum_ref, pair_land, right_land, left_land, right_sum, left_sum, ys, yr, rs, rr, ls, lr
+):
     me_dp, me_neg = lax.axis_index("dp"), lax.axis_index("neg")
+    line = ndp // 2
+    place, side = me_dp // 2, lax.rem(me_dp, 2)
+    partner = me_dp + 1 - 2 * side
+    cuts = part_ref.shape[1]
     greet(ndp, 1, me_dp, me_neg)
-    copies = share("dp", ndp, me_dp, lambda t: part_ref.at[t], land, ns, nr)
-    finish(copies)
-    result = part_ref[me_dp].astype(jnp.float32)
-    for k in range(1, ndp):
-        result = result + land[lax.rem(me_dp + k, ndp)].astype(jnp.float32)
-    sum_ref[...] = result
+    order = sorted(range(line), key=lambda z: -abs(2 * z - line + 1))
+    steps = [(z, j) for z in order for j in range(cuts)]
+    from_left, from_right = place > 0, place < line - 1
+
+    def across(z, j):
+        return link(part_ref.at[2 * z + 1 - side, j], pair_land.at[z, j], (ys, yr), z * cuts + j, "dp", partner)
+
+    def right(z, j):
+        return link(right_sum.at[z, j], right_land.at[z, j], (rs, rr), z * cuts + j, "dp", lax.rem(me_dp + 2, ndp))
+
+    def left(z, j):
+        return link(left_sum.at[z, j], left_land.at[z, j], (ls, lr), z * cuts + j, "dp", lax.rem(me_dp + ndp - 2, ndp))
+
+    for z, j in steps:
+        across(z, j).start()
+    for z, j in steps:
+        across(z, j).wait_recv()
+        own = part_ref[2 * z + side, j].astype(jnp.float32) + pair_land[z, j].astype(jnp.float32)
+
+        @pl.when(place == z)
+        def _():
+            sum_ref[j] = own
+
+        @pl.when(place == 0 if z else False)
+        def _():
+            right_sum[z, j] = own.astype(jnp.bfloat16)
+
+        @pl.when((place > 0) & (place < z))
+        def _():
+            right(z, j).wait_recv()
+            right_sum[z, j] = (own + right_land[z, j].astype(jnp.float32)).astype(jnp.bfloat16)
+
+        pl.when(place < z)(lambda: right(z, j).start())
+
+        @pl.when(place == line - 1 if z < line - 1 else False)
+        def _():
+            left_sum[z, j] = own.astype(jnp.bfloat16)
+
+        @pl.when((place < line - 1) & (place > z))
+        def _():
+            left(z, j).wait_recv()
+            left_sum[z, j] = (own + left_land[z, j].astype(jnp.float32)).astype(jnp.bfloat16)
+
+        pl.when(place > z)(lambda: left(z, j).start())
+
+    for j in range(cuts):
+
+        @pl.when(from_left)
+        def _():
+            right(place, j).wait_recv()
+            sum_ref[j] = sum_ref[j] + right_land[place, j].astype(jnp.float32)
+
+        @pl.when(from_right)
+        def _():
+            left(place, j).wait_recv()
+            sum_ref[j] = sum_ref[j] + left_land[place, j].astype(jnp.float32)
+
+    for z, j in steps:
+        across(z, j).wait_send()
+        pl.when(place < z)(lambda: right(z, j).wait_send())
+        pl.when(place > z)(lambda: left(z, j).wait_send())
 
 
 def weight_kernel(
     ndp, nneg, packed_ref, loss_ref, gathered_ref, stats_ref,
-    core_land, core_sum, row_land, row_sum, dp_land, stat_dp, stat_dp_land, stat_neg, stat_neg_land,
-    cs, cr, xs, xr, ps, pr, ss, sr, ts, tr, gs, gr,
+    core_land, sum_a, sum_b, land_a, land_b, half_a, half_b, last_a, last_b, line_sum, line_land,
+    stat_dp, stat_dp_land, stat_neg, stat_neg_land,
+    cs, cr, xs, xr, ys, yr, ps, pr, ss, sr, ts, tr, gs, gr, hs, hr,
 ):
     me_dp, me_neg = lax.axis_index("dp"), lax.axis_index("neg")
-    nx = nneg // 2
+    nx, line = nneg // 2, ndp // 2
     me_x, me_core = me_neg // 2, lax.rem(me_neg, 2)
-    other = 1 - me_core
+    place, side = me_dp // 2, lax.rem(me_dp, 2)
+    other, far = 1 - me_core, 1 - side
+    mate, partner = 2 * me_x + other, 2 * place + far
     greet(ndp, nneg, me_dp, me_neg)
-    core = [
-        send(packed_ref.at[2 * x + other], core_land.at[x], cs.at[x], cr.at[x], "neg", 2 * me_x + other)
-        for x in range(nx)
-    ]
-    row = []
-    for k in list(range(1, nx)) + [0]:
-        x = lax.rem(me_x + k, nx)
-        if k == 1 or nx == 1:
-            finish(core)
-
-        def core_add(d, carry):
-            core_sum[x, d] = (
-                packed_ref[2 * x + me_core, d].astype(jnp.float32) + core_land[x, d].astype(jnp.float32)
+    turn = list(range(1, nx)) + [0]
+
+    def x_of(k):
+        return lax.rem(me_x + k, nx)
+
+    core = {}
+    for k in turn:
+        x = x_of(k)
+        core[k] = send(packed_ref.at[2 * x + other], core_land.at[x], cs.at[k], cr.at[k], "neg", mate)
+
+    def add_core(x, y, half, target):
+        def body(z, carry):
+            target[z] = (
+                packed_ref[2 * x + me_core, 2 * z + y, half].astype(jnp.float32)
+                + core_land[x, 2 * z + y, half].astype(jnp.float32)
             ).astype(jnp.bfloat16)
             return carry
 
-        lax.fori_loop(0, ndp, core_add, 0)
+        lax.fori_loop(0, line, body, 0)
+
+    def add(target, *terms):
+        def body(z, carry):
+            value = terms[0][z].astype(jnp.float32)
+            for term in terms[1:]:
+                value = value + term[z].astype(jnp.float32)
+            target[z] = value.astype(jnp.bfloat16)
+            return carry
+
+        lax.fori_loop(0, line, body, 0)
+
+    first_a = []
+    for k in turn:
+        x = x_of(k)
+        core[k].wait_recv()
         if k:
-            row.append(
-                send(core_sum.at[x], row_land.at[k], xs.at[k], xr.at[k], "neg", 2 * x + me_core)
+            for y in range(2):
+                add_core(x, y, 0, sum_a.at[x, y])
+            first_a.append(send(sum_a.at[x], land_a.at[k], xs.at[k], xr.at[k], "neg", 2 * x + me_core))
+        add_core(x, far, 1, sum_b.at[far, x])
+    first_b = send(sum_b.at[far], land_b, ys.at[0], yr.at[0], "dp", partner)
+    for y in range(2):
+        add_core(me_x, y, 0, sum_a.at[me_x, y])
+    for k in range(nx):
+        add_core(x_of(k), side, 1, sum_b.at[side, x_of(k)])
+    for copy in first_a:
+        copy.wait_recv()
+    add(half_a.at[far], sum_a.at[me_x, far], *[land_a.at[k, far] for k in range(1, nx)])
+    second_a = send(half_a.at[far], last_a, ys.at[1], yr.at[1], "dp", partner)
+    first_b.wait_recv()
+    second_b = []
+    for k in turn:
+        x = x_of(k)
+        add(half_b.at[x], sum_b.at[side, x], land_b.at[x])
+        if k:
+            second_b.append(
+                send(half_b.at[x], last_b.at[k], xs.at[nx + k], xr.at[nx + k], "neg", 2 * x + me_core)
             )
-    finish(row)
-
-    def row_add(d, carry):
-        value = core_sum[me_x, d].astype(jnp.float32)
-        for k in range(1, nx):
-            value = value + row_land[k, d].astype(jnp.float32)
-        row_sum[d] = value.astype(jnp.bfloat16)
-        return carry
-
-    lax.fori_loop(0, ndp, row_add, 0)
-    finish(share("dp", ndp, me_dp, lambda t: row_sum.at[t], dp_land, ps, pr))
-    piece = row_sum[me_dp].astype(jnp.float32)
-    for k in range(1, ndp):
-        piece = piece + dp_land[lax.rem(me_dp + k, ndp)].astype(jnp.float32)
-    gathered_ref[me_neg] = piece.astype(jnp.bfloat16)
+    add(half_a.at[side], sum_a.at[me_x, side], *[land_a.at[k, side] for k in range(1, nx)])
+    second_a.wait_recv()
+    add(line_sum.at[0], half_a.at[side], last_a)
+    third = []
+    for half in range(2):
+        if half:
+            for copy in second_b:
+                copy.wait_recv()
+            add(line_sum.at[1], half_b.at[me_x], *[last_b.at[k] for k in range(1, nx)])
+        for k in range(1, line):
+            z = lax.rem(place + k, line)
+            third.append(
+                send(line_sum.at[half, z], line_land.at[half, k], ps.at[half * line + k], pr.at[half * line + k], "dp", 2 * z + side)
+            )
+    for copy in third:
+        copy.wait_recv()
+    squares = jnp.zeros((), jnp.float32)
+    for half in range(2):
+        piece = line_sum[half, place].astype(jnp.float32)
+        for k in range(1, line):
+            piece = piece + line_land[half, k].astype(jnp.float32)
+        gathered_ref[me_neg, half] = piece.astype(jnp.bfloat16)
+        squares = squares + jnp.sum(piece * piece)
     lane = lax.broadcasted_iota(jnp.int32, (8, 128), 1)
-    stat_dp[...] = jnp.where(lane == 0, jnp.sum(piece * piece), loss_ref[0])
+    stat_dp[...] = jnp.where(lane == 0, squares, loss_ref[0])
     stat_copies = share("dp", ndp, me_dp, lambda t: stat_dp, stat_dp_land, ss, sr)
-    gather = share("neg", nneg, me_neg, lambda t: gathered_ref.at[me_neg], gathered_ref, gs, gr)
+    mine = gathered_ref.at[me_neg]
+    spread = [send(mine, mine, gs.at[k], gr.at[k], "neg", 2 * x_of(k) + me_core) for k in range(1, nx)]
+    spread.append(send(mine, mine, gs.at[0], gr.at[0], "neg", mate))
     finish(stat_copies)
     total = stat_dp[...]
     for k in range(1, ndp):
         total = total + stat_dp_land[lax.rem(me_dp + k, ndp)]
     stat_neg[...] = total
-    finish(share("neg", nneg, me_neg, lambda t: stat_neg, stat_neg_land, ts, tr))
+    stat_copies = share("neg", nneg, me_neg, lambda t: stat_neg, stat_neg_land, ts, tr)
+    relay = []
+    for k in range(1, nx):
+        spread[k - 1].wait_recv()
+        x = lax.rem(me_x + nx - k, nx)
+        came = gathered_ref.at[2 * x + me_core]
+        relay.append(send(came, came, hs.at[k], hr.at[k], "neg", mate))
+    finish(stat_copies)
     total = stat_neg[...]
     for k in range(1, nneg):
         total = total + stat_neg_land[lax.rem(me_neg + k, nneg)]
     stats_ref[...] = total
-    finish(gather)
+    spread[-1].wait_recv()
+    finish(relay)
+    for copy in [*core.values(), *first_a, first_b, second_a, *second_b, *third, *spread]:
+        copy.wait_send()
 
 
 def call(kernel, collective, ndp, nneg, out_shape, scratch, in_specs):
@@ -242,6 +434,8 @@
     negative_unit = item_unit[own_rows:]
     ndp, nneg = lax.axis_size("dp"), lax.axis_size("neg")
     width = query_unit.shape[1]
+    cuts = 2
+    cut_rows = negative_unit.shape[0] // cuts
     group_unit, shard_unit = call(
         gather_kernel,
         0,
@@ -249,11 +443,11 @@
         nneg,
         (
             jax.ShapeDtypeStruct((nneg,) + query_unit.shape, jnp.bfloat16),
-            jax.ShapeDtypeStruct((ndp,) + negative_unit.shape, jnp.bfloat16),
+            jax.ShapeDtypeStruct((ndp, cuts, cut_rows, width), jnp.bfloat16),
         ),
-        sems(nneg, nneg, ndp, ndp),
+        sems(nneg, nneg, *([ndp // 2 * cuts + cuts] * 4), *([ndp * cuts] * 2)),
         [vmem, vmem],
-    )(query_unit, negative_unit)
+    )(query_unit, negative_unit.reshape(cuts, cut_rows, width))
     group_unit = group_unit.reshape(-1, width)
     shard_unit = shard_unit.reshape(-1, width)
     scores = (
@@ -295,16 +489,18 @@
     query_sum = query_total / own_denom[:, None]
     scaled_unit = (group_unit.astype(jnp.float32) / denom[:, None]).astype(jnp.bfloat16)
     negative_part = contract_rows(block, scaled_unit).astype(jnp.bfloat16)
-    negative_rows = negative_unit.shape[0]
+    line = ndp // 2
+    cut = (cuts, cut_rows, width)
     (negative_sum,) = call(
         negative_kernel,
         2,
         ndp,
         nneg,
-        (jax.ShapeDtypeStruct((negative_rows, width), jnp.float32),),
-        [pltpu.VMEM((ndp, negative_rows, width), jnp.bfloat16)] + sems(ndp, ndp),
+        (jax.ShapeDtypeStruct(cut, jnp.float32),),
+        [pltpu.VMEM((line,) + cut, jnp.bfloat16)] * 5 + sems(*([line * cuts] * 6)),
         [vmem],
-    )(negative_part.reshape(ndp, negative_rows, width))
+    )(negative_part.reshape((ndp,) + cut))
+    negative_sum = negative_sum.reshape(negative_unit.shape)
     query_grad = (
         query_sum + positive_slope[:, None] * positive_unit.astype(jnp.float32)
     ) * inv_temp
@@ -316,28 +512,34 @@
     parts = [part for gradient in gradients for part in to_packed(gradient, ndp)]
     packed = jnp.concatenate(parts, axis=1)
     rows = packed.shape[1] // nneg
-    packed = packed.reshape(ndp, nneg, rows, pack_columns).transpose(1, 0, 2, 3)
+    packed = packed.reshape(ndp, nneg, 2, rows // 2, pack_columns).transpose(1, 0, 2, 3, 4)
     nx = nneg // 2
-    piece = (rows, pack_columns)
+    piece = (rows // 2, pack_columns)
     bf16, f32 = jnp.bfloat16, jnp.float32
     gathered, stats = call(
         weight_kernel,
         3,
         ndp,
         nneg,
-        (jax.ShapeDtypeStruct((nneg,) + piece, bf16), jax.ShapeDtypeStruct((8, 128), f32)),
+        (jax.ShapeDtypeStruct((nneg, 2) + piece, bf16), jax.ShapeDtypeStruct((8, 128), f32)),
         [
-            pltpu.VMEM((nx, ndp) + piece, bf16),
-            pltpu.VMEM((nx, ndp) + piece, bf16),
-            pltpu.VMEM((nx, ndp) + piece, bf16),
-            pltpu.VMEM((ndp,) + piece, bf16),
-            pltpu.VMEM((ndp,) + piece, bf16),
+            pltpu.VMEM((nx, ndp, 2) + piece, bf16),
+            pltpu.VMEM((nx, 2, line) + piece, bf16),
+            pltpu.VMEM((2, nx, line) + piece, bf16),
+            pltpu.VMEM((nx, 2, line) + piece, bf16),
+            pltpu.VMEM((nx, line) + piece, bf16),
+            pltpu.VMEM((2, line) + piece, bf16),
+            pltpu.VMEM((nx, line) + piece, bf16),
+            pltpu.VMEM((line,) + piece, bf16),
+            pltpu.VMEM((nx, line) + piece, bf16),
+            pltpu.VMEM((2, line) + piece, bf16),
+            pltpu.VMEM((2, line) + piece, bf16),
             pltpu.VMEM((8, 128), f32),
             pltpu.VMEM((ndp, 8, 128), f32),
             pltpu.VMEM((8, 128), f32),
             pltpu.VMEM((nneg, 8, 128), f32),
         ]
-        + sems(nx, nx, nx, nx, ndp, ndp, ndp, ndp, nneg, nneg, nneg, nneg),
+        + sems(nx, nx, 2 * nx, 2 * nx, 2, 2, ndp, ndp, ndp, ndp, nneg, nneg, nx, nx, nx, nx),
         [vmem, pl.BlockSpec(memory_space=pltpu.SMEM)],
     )(packed, loss_part.reshape(1))
     grad_norm = jnp.sqrt(stats[0, 0])

time: 236 us -> 178 us (0.75)
  Pallas kernels: 182 us -> 125 us
    pallas_call x2, Pallas kernels: 134 us -> 87 us  [the longest x1 56.9 us: per_device(): call(weight_kernel, 3, ndp, nneg, (jax.ShapeDtypeStruct((nneg, 2) + piece...]
    pallas_call x1, Pallas kernels: 40 us -> 30.2 us  [per_device(): call(gather_kernel, 0, ndp, nneg, (jax.ShapeDtypeStruct((nneg,) + query_u...]
    unnamed x82 -> x88, local copies, waits for them, and re-layouts: 4.57 us -> 5.03 us
where the time goes in v2:
time: 178 us
  Pallas kernels  125 us (70%)
  matrix products  36 us (20%)
  local copies, waits for them, and re-layouts  7.26 us (4%)
  other arithmetic  5.23 us (3%)
  between operations  3.81 us (2%)
    pallas_call x1, Pallas kernels, per_device(): call(weight_kernel, 3, ndp, nneg, (jax.ShapeDtypeStruct((nneg, 2) + piece...  56.9 us
    pallas_call x1, Pallas kernels, per_device(): call(gather_kernel, 0, ndp, nneg, (jax.ShapeDtypeStruct((nneg,) + query_u...  30.2 us
    pallas_call x1, Pallas kernels, per_device(): call(negative_kernel, 2, ndp, nneg, (jax.ShapeDtypeStruct(cut, jnp.float3...  30.1 us
    dot_general x7, matrix products, contract_rows(): lax.dot_general(left, right, (((0,), (0,)), ((), ())), preferred_element_...  17.3 us
    dot_general x3, matrix products, contract_cols(): lax.dot_general(left, right, (((1,), (1,)), ((), ())), preferred_element_...  8.78 us
    pallas_call x1, Pallas kernels, per_device(): call(query_kernel, 1, ndp, nneg, (jax.ShapeDtypeStruct((own_rows, width),...  8.02 us
    unnamed x88, local copies, waits for them, and re-layouts  5.03 us

profile of v2, /device:TPU:0, one launch (start us, length us, event | category | flops | bytes accessed | tf_op | source)
XLA Modules:
  0.0 177.6 jit_solution(14360685111970521574)
XLA Ops:
  0.6 0.0 copy-start
  0.6 1.1 constant_dynamic-update-slice_fusion.1
  1.7 1.1 constant_dynamic-update-slice_fusion
  2.8 2.9 %multiply_convert_fusion.1 = (bf16[768,1024]{1,0:T(8,128)(2,1)S(1)}, f32[768,1024]{1,0:T(8,128)}) fusion(bf16[768,512]{1,0:T(8,128)(2,1)S(1)} %constant_dynamic-update-slice_fusion, bf16[512,1024]{1,0:T(8,128)(2,1)S(1)} %copy-done), kind=kOutput, calls=%fused_computation.6 | convolution fusion | flops 809238528 | bytes 6553600 | tf_op jit(solution)/shard_map/dot_general | solution.py:32
  5.7 2.3 %multiply_convert_fusion.3 = (bf16[768,512]{1,0:T(8,128)(2,1)S(1)}, f32[768,512]{1,0:T(8,128)}) fusion(bf16[768,1024]{1,0:T(8,128)(2,1)S(1)} %get-tuple-element.50, bf16[1024,512]{1,0:T(8,128)(2,1)S(1)} %copy-done.28), kind=kOutput, calls=%fused_computation.9 | convolution fusion | flops 807272448 | bytes 4980736 | tf_op jit(solution)/shard_map/dot_general | solution.py:34
  8.0 0.4 multiply_reduce_fusion.1
  8.5 0.4 copy-done.9
  8.9 0.2 multiply_convert_fusion.5
  9.1 0.4 copy-done.3
  9.5 0.0 copy-done.15
  9.5 0.4 fusion.19
  10.1 1.3 multiply_convert_fusion.6
  11.3 0.3 multiply_reduce_fusion.3
  11.6 0.4 copy-done.7
  12.0 0.1 copy.23
  12.2 0.6 broadcast_multiply_fusion.1
  12.8 0.2 fusion.11
  13.0 30.2 %shard_map.180 = (bf16[4,256,256]{2,1,0:T(8,128)(2,1)S(1)}, bf16[8,2,256,256]{3,2,1,0:T(8,128)(2,1)S(1)}) custom-call(bf16[256,256]{1,0:T(8,128)(2,1)S(1)} %get-tuple-element.22.query_ref, bf16[2,256,256]{2,1,0:T(8,128)(2,1)S(1)} %bitcast.59), custom_call_target="tpu_custom_call" | custom-call | tf_op jit(solution)/shard_map/pallas_call | solution.py:439
  43.3 5.1 %fusion = (f32[1024]{0:T(1024)S(1)}, bf16[1024,4096]{1,0:T(8,128)(2,1)S(1)}) fusion(f32[4096]{0:T(1024)S(1)} %convert_log_fusion, s32[4096]{0:T(1024)S(1)} %copy-done.30, s32[1024]{0:T(1024)S(1)} %copy-done.31, bf16[1024,256]{1,0:T(8,128)(2,1)S(1)} %bitcast.69, bf16[4096,256]{1,0:T(8,128)(2,1)S(1)} %bitcast.67), kind=kOutput, calls=%fused_computation.1 | convolution fusion | flops 2172648448 | bytes 11051008 | tf_op jit(solution)/shard_map/dot_general | solution.py:26
  48.4 2.3 %convolution_convert_fusion.5 = bf16[1024,256]{1,0:T(8,128)(2,1)S(1)} fusion(bf16[1024,4096]{1,0:T(8,128)(2,1)S(1)} %get-tuple-element.24, bf16[4096,256]{1,0:T(8,128)(2,1)S(1)} %bitcast.68), kind=kOutput, calls=%fused_computation.16 | convolution fusion | flops 2147745792 | bytes 11010048 | tf_op jit(solution)/shard_map/dot_general | solution.py:467
  50.7 0.9 copy-done.32
  51.7 0.1 add_dynamic-update-slice_fusion
  51.8 8.0 %shard_map.181 = (f32[256,256]{1,0:T(8,128)S(1)}, f32[8,128]{1,0:T(8,128)S(1)}) custom-call(bf16[4,256,256]{2,1,0:T(8,128)(2,1)S(1)} %bitcast.63, f32[8,128]{1,0:T(8,128)S(1)} %bitcast.64), custom_call_target="tpu_custom_call" | custom-call | tf_op jit(solution)/shard_map/pallas_call | solution.py:469
  59.8 5.9 %convolution_convert_fusion = bf16[4096,256]{1,0:T(8,128)(2,1)S(1)} fusion(bf16[1024,4096]{1,0:T(8,128)(2,1)} %copy-done.32, bf16[1024,256]{1,0:T(8,128)(2,1)S(1)} %bitcast.70, f32[1024]{0:T(1024)S(1)} %bitcast.65), kind=kOutput, calls=%fused_computation.3 | convolution fusion | flops 2149318656 | bytes 11014144 | tf_op jit(solution)/shard_map/dot_general | solution.py:20
  65.8 30.1 %shard_map.182 = f32[2,256,256]{2,1,0:T(8,128)S(1)} custom-call(bf16[8,2,256,256]{3,2,1,0:T(8,128)(2,1)S(1)} %bitcast.58), custom_call_target="tpu_custom_call" | custom-call | tf_op jit(solution)/shard_map/pallas_call | solution.py:494
  96.0 0.7 subtract_reduce_fusion
  96.7 0.2 fusion.10
  97.0 0.2 multiply_reduce_fusion
  97.2 0.4 subtract_convert_fusion
  97.6 1.6 multiply_convert_fusion.2
  99.3 5.5 %convolution_convert_fusion.2 = bf16[512,1024]{1,0:T(8,128)(2,1)} fusion(bf16[768,512]{1,0:T(8,128)(2,1)S(1)} %copy-done.20, f32[768,1024]{1,0:T(8,128)} %get-tuple-element.51, bf16[768,512]{1,0:T(8,128)(2,1)} %multiply_convert_fusion.2, bf16[1024,512]{1,0:T(8,128)(2,1)} %param.24), kind=kOutput, calls=%fused_computation.12 | convolution fusion | flops 1618214912 | bytes 6815744 | tf_op jit(solution)/shard_map/dot_general | solution.py:20
  104.8 0.2 subtract_convert_fusion.1
  105.1 2.1 %fusion.3 = bf16[256,512]{1,0:T(8,128)(2,1)} fusion(bf16[256,256]{1,0:T(8,128)(2,1)S(1)} %subtract_convert_fusion.1, bf16[512,256]{1,0:T(8,128)(2,1)S(1)} %copy-done.18, f32[256,512]{1,0:T(8,128)} %get-tuple-element.49), kind=kOutput, calls=%fused_computation.21 | convolution fusion | flops 68288512 | bytes 1179648 | tf_op jit(solution)/shard_map/dot_general | solution.py:26
  107.1 2.6 %convolution_convert_fusion.4 = bf16[1024,512]{0,1:T(8,128)(2,1)S(1)} fusion(bf16[256,512]{1,0:T(8,128)(2,1)S(1)} %copy-done.16, bf16[256,512]{1,0:T(8,128)(2,1)} %fusion.3, bf16[1024,512]{1,0:T(8,128)(2,1)} %param.21, f32[256,1024]{1,0:T(8,128)} %copy-done.4), kind=kOutput, calls=%fused_computation.14 | convolution fusion | flops 539754496 | bytes 3670016 | tf_op jit(solution)/shard_map/dot_general | solution.py:20
  110.0 1.6 convolution_convert_fusion.3
  111.6 0.3 convolution_convert_fusion.7
  112.1 0.8 copy-done.34
  112.9 0.2 copy-done.35
  113.1 1.0 convolution_convert_fusion.1
  114.2 0.0 copy-done.10
  114.3 0.1 copy-done.12
  114.4 0.4 convolution_convert_fusion.6
  114.8 0.3 copy.28
  115.1 56.9 %shard_map.183 = (bf16[4,2,144,256]{3,2,1,0:T(8,128)(2,1)S(1)}, f32[8,128]{1,0:T(8,128)S(1)}) custom-call(bf16[4,8,2,144,256]{4,3,2,1,0:T(8,128)(2,1)S(1)} %bitcast.57, f32[1]{0:T(128)} %bitcast.18.loss_ref), custom_call_target="tpu_custom_call" | custom-call | tf_op jit(solution)/shard_map/pallas_call | solution.py:519
  172.0 0.6 fusion.18
  173.4 0.7 convert_multiply_fusion.7
  174.1 0.9 convert_multiply_fusion.3
  175.0 0.8 convert_multiply_fusion.4
  (85 shorter events, 0.8 us)
Async XLA Ops:
  0.6 2.2 %copy-start = (bf16[512,1024]{1,0:T(8,128)(2,1)S(1)}, bf16[512,1024]{1,0:T(8,128)(2,1)}, u32[]{:S(2)}) copy-start(bf16[512,1024]{1,0:T(8,128)(2,1)} %param.23) | copy-start | bytes 3145732
  2.8 2.9 %copy-start.19 = (bf16[768,512]{1,0:T(8,128)(2,1)}, bf16[768,512]{1,0:T(8,128)(2,1)S(1)}, u32[]{:S(2)}) copy-start(bf16[768,512]{1,0:T(8,128)(2,1)S(1)} %constant_dynamic-update-slice_fusion) | copy-start | bytes 2359300
  2.8 2.9 %copy-start.28 = (bf16[1024,512]{1,0:T(8,128)(2,1)S(1)}, bf16[1024,512]{1,0:T(8,128)(2,1)}, u32[]{:S(2)}) copy-start(bf16[1024,512]{1,0:T(8,128)(2,1)} %param.24) | copy-start | bytes 3145732
  5.7 2.3 %copy-start.33 = (bf16[768,1024]{1,0:T(8,128)(2,1)}, bf16[768,1024]{1,0:T(8,128)(2,1)S(1)}, u32[]{:S(2)}) copy-start(bf16[768,1024]{1,0:T(8,128)(2,1)S(1)} %get-tuple-element.50) | copy-start | bytes 4718596
  5.7 2.3 %copy-start.13 = (bf16[512,256]{1,0:T(8,128)(2,1)S(1)}, bf16[512,256]{1,0:T(8,128)(2,1)}, u32[]{:S(2)}) copy-start(bf16[512,256]{1,0:T(8,128)(2,1)} %param.25) | copy-start | bytes 786436
  8.0 0.9 copy-start.9
  8.0 1.5 copy-start.3
  8.0 1.5 copy-start.15
  8.0 2.0 %copy-start.29 = (bf16[1024,512]{1,0:T(8,128)(2,1)S(1)}, bf16[1024,512]{1,0:T(8,128)(2,1)}, u32[]{:S(2)}) copy-start(bf16[1024,512]{1,0:T(8,128)(2,1)} %param.21) | copy-start | bytes 3145732
  9.5 3.4 %copy-start.1 = (bf16[768,256]{1,0:T(8,128)(2,1)}, bf16[768,256]{1,0:T(8,128)(2,1)S(1)}, u32[]{:S(2)}) copy-start(bf16[768,256]{1,0:T(8,128)(2,1)S(1)} %multiply_convert_fusion.5) | copy-start | bytes 1179652
  10.0 1.3 copy-start.4
  10.0 1.3 copy-start.17
  10.0 33.2 %copy-start.21 = (s32[4096]{0:T(1024)S(1)}, s32[4096]{0:T(1024)}, u32[]{:S(2)}) copy-start(s32[4096]{0:T(1024)} %param.19) | copy-start | bytes 49156
  10.0 33.2 %copy-start.30 = (s32[4096]{0:T(1024)S(1)}, s32[4096]{0:T(1024)}, u32[]{:S(2)}) copy-start(s32[4096]{0:T(1024)} %param.18) | copy-start | bytes 49156
  10.0 33.2 %copy-start.31 = (s32[1024]{0:T(1024)S(1)}, s32[1024]{0:T(1024)}, u32[]{:S(2)}) copy-start(s32[1024]{0:T(1024)} %param.16) | copy-start | bytes 12292
  11.3 0.7 copy-start.7
  48.4 3.3 %copy-start.32 = (bf16[1024,4096]{1,0:T(8,128)(2,1)}, bf16[1024,4096]{1,0:T(8,128)(2,1)S(1)}, u32[]{:S(2)}) copy-start(bf16[1024,4096]{1,0:T(8,128)(2,1)S(1)} %get-tuple-element.24) | copy-start | bytes 25165828
  48.4 3.3 %copy-start.24 = (s32[256]{0:T(256)S(1)}, s32[256]{0:T(256)}, u32[]{:S(2)}) copy-start(s32[256]{0:T(256)} %param.17) | copy-start | bytes 3076
  65.8 30.2 %copy-start.25 = (s32[256]{0:T(256)S(1)}, s32[256]{0:T(256)}, u32[]{:S(2)}) copy-start(s32[256]{0:T(256)} %param.17) | copy-start | bytes 3076
  65.8 30.9 %copy-start.2 = (bf16[768,256]{1,0:T(8,128)(2,1)S(1)}, bf16[768,256]{1,0:T(8,128)(2,1)}, u32[]{:S(2)}) copy-start(bf16[768,256]{1,0:T(8,128)(2,1)} %copy-done.1) | copy-start | bytes 1179652
  96.0 1.6 copy-start.14
  96.0 1.6 copy-start.36
  96.7 2.5 %copy-start.22 = (f32[256]{0:T(256)}, f32[256]{0:T(256)S(1)}, u32[]{:S(2)}) copy-start(f32[256]{0:T(256)S(1)} %divide_add_fusion) | copy-start | bytes 3076
  97.6 1.7 copy-start.11
  97.6 1.6 copy-start.20
  99.2 5.6 %copy-start.23 = (f32[256]{0:T(256)S(1)}, f32[256]{0:T(256)}, u32[]{:S(2)}) copy-start(f32[256]{0:T(256)} %copy-done.22) | copy-start | bytes 3076
  99.2 5.6 %copy-start.26 = (f32[256]{0:T(256)S(1)}, f32[256]{0:T(256)}, u32[]{:S(2)}) copy-start(f32[256]{0:T(256)} %get-tuple-element.45) | copy-start | bytes 3076
  99.2 5.6 %copy-start.27 = (f32[256]{0:T(256)S(1)}, f32[256]{0:T(256)}, u32[]{:S(2)}) copy-start(f32[256]{0:T(256)} %get-tuple-element.46) | copy-start | bytes 3076
  99.2 5.8 %copy-start.18 = (bf16[512,256]{1,0:T(8,128)(2,1)S(1)}, bf16[512,256]{1,0:T(8,128)(2,1)}, u32[]{:S(2)}) copy-start(bf16[512,256]{1,0:T(8,128)(2,1)} %param.22) | copy-start | bytes 786436
  104.8 2.3 %copy-start.16 = (bf16[256,512]{1,0:T(8,128)(2,1)S(1)}, bf16[256,512]{1,0:T(8,128)(2,1)}, u32[]{:S(2)}) copy-start(bf16[256,512]{1,0:T(8,128)(2,1)} %param.13) | copy-start | bytes 786436
  107.1 2.8 %copy-start.5 = (f32[256,1024]{1,0:T(8,128)S(1)}, f32[256,1024]{1,0:T(8,128)}, u32[]{:S(2)}) copy-start(f32[256,1024]{1,0:T(8,128)} %copy-done.4) | copy-start | bytes 3145732
  109.9 1.7 copy-start.8
  109.9 2.0 %copy-start.6 = (bf16[512,1024]{1,0:T(8,128)(2,1)S(1)}, bf16[512,1024]{1,0:T(8,128)(2,1)}, u32[]{:S(2)}) copy-start(bf16[512,1024]{1,0:T(8,128)(2,1)} %convolution_convert_fusion.2) | copy-start | bytes 3145732
  111.5 1.4 copy-start.34
  111.5 1.6 copy-start.35
  113.1 1.1 copy-start.10
  113.1 1.2 copy-start.12

commit v3 on v2

--- a/solution.py
+++ b/solution.py
@@ -114,65 +114,78 @@
     line = ndp // 2
     place = me_dp // 2
     partner = me_dp + 1 - 2 * lax.rem(me_dp, 2)
-    cuts = negative_ref.shape[0]
     greet(ndp, nneg, me_dp, me_neg)
     goes_right, goes_left = place < line - 1, place > 0
 
-    def block(slot, j, distance):
-        return negative_ref.at[j] if distance == 0 else shard_ref.at[slot, j]
-
-    def right(distance, j):
-        slot = me_dp - 2 * distance
-        return link(block(slot, j, distance), shard_ref.at[slot, j], (rs, rr), (distance + 1) * cuts + j, "dp", lax.rem(me_dp + 2, ndp))
-
-    def left(distance, j):
-        slot = me_dp + 2 * distance
-        return link(block(slot, j, distance), shard_ref.at[slot, j], (ls, lr), (distance + 1) * cuts + j, "dp", lax.rem(me_dp + ndp - 2, ndp))
-
-    def across(offset, j):
-        slot = me_dp + 2 * offset
-        return link(block(slot, j, abs(offset)), shard_ref.at[slot, j], (ys, yr), (offset + line - 1) * cuts + j, "dp", partner)
-
-    def arrival(slot, j, sems, index):
-        return link(shard_ref.at[slot, j], shard_ref.at[slot, j], sems, index, "dp", partner)
-
-    for j in range(cuts):
-        pl.when(goes_right)(lambda j=j: right(0, j).start())
-        pl.when(goes_left)(lambda j=j: left(0, j).start())
-        across(0, j).start()
+    def at(lane, offset):
+        slot = (partner if lane == 2 else me_dp) + 2 * offset
+        return shard_ref.at[slot, min(lane, 1)]
+
+    def source(lane, offset):
+        return negative_ref.at[lane] if offset == 0 and lane < 2 else at(lane, offset)
+
+    def right(lane, distance):
+        return link(source(lane, -distance), at(lane, -distance), (rs, rr), (distance + 1) * 3 + lane, "dp", lax.rem(me_dp + 2, ndp))
+
+    def left(lane, distance):
+        return link(source(lane, distance), at(lane, distance), (ls, lr), (distance + 1) * 3 + lane, "dp", lax.rem(me_dp + ndp - 2, ndp))
+
+    def across(offset):
+        return link(source(0, offset), at(0, offset), (ys, yr), offset + line - 1, "dp", partner)
+
+    def across_second():
+        return link(negative_ref.at[1], at(1, 0), (ys, yr), 2 * line - 1, "dp", partner)
+
+    def arrival(ref, sems, index):
+        return link(ref, ref, sems, index, "dp", partner)
+
+    def begin(lane):
+        pl.when(goes_right)(lambda: right(lane, 0).start())
+        pl.when(goes_left)(lambda: left(lane, 0).start())
+
+    across_second().start()
+    begin(0)
+    begin(1)
+    across(0).start()
     copies = share("neg", nneg, me_neg, lambda t: query_ref, group_ref, qs, qr)
     group_ref[me_neg] = query_ref[...]
     shard_ref[me_dp] = negative_ref[...]
+    arrival(at(2, 0), (ys, yr), 2 * line - 1).wait_recv()
+    begin(2)
     for distance in range(1, line):
-        for j in range(cuts):
+        for lane in range(3):
 
             @pl.when(place >= distance)
             def _():
-                arrival(me_dp - 2 * distance, j, (rs, rr), distance * cuts + j).wait_recv()
-                across(-distance, j).start()
-                pl.when(goes_right)(lambda: right(distance, j).start())
+                arrival(at(lane, -distance), (rs, rr), distance * 3 + lane).wait_recv()
+                if lane == 0:
+                    across(-distance).start()
+                pl.when(goes_right)(lambda: right(lane, distance).start())
 
             @pl.when(place + distance < line)
             def _():
-                arrival(me_dp + 2 * distance, j, (ls, lr), distance * cuts + j).wait_recv()
-                across(distance, j).start()
-                pl.when(goes_left)(lambda: left(distance, j).start())
-
+                arrival(at(lane, distance), (ls, lr), distance * 3 + lane).wait_recv()
+                if lane == 0:
+                    across(distance).start()
+                pl.when(goes_left)(lambda: left(lane, distance).start())
+
+    across_second().wait_send()
     for distance in range(line):
-        for j in range(cuts):
-
-            @pl.when(place >= distance)
-            def _():
-                across(-distance, j).wait_send()
-                arrival(partner - 2 * distance, j, (ys, yr), (line - 1 - distance) * cuts + j).wait_recv()
-                pl.when(goes_right)(lambda: right(distance, j).wait_send())
-
-            @pl.when(place + distance < line)
-            def _():
-                if distance:
-                    across(distance, j).wait_send()
-                    arrival(partner + 2 * distance, j, (ys, yr), (line - 1 + distance) * cuts + j).wait_recv()
-                pl.when(goes_left)(lambda: left(distance, j).wait_send())
+
+        @pl.when(place >= distance)
+        def _():
+            across(-distance).wait_send()
+            arrival(shard_ref.at[partner - 2 * distance, 0], (ys, yr), line - 1 - distance).wait_recv()
+            for lane in range(3):
+                pl.when(goes_right)(lambda: right(lane, distance).wait_send())
+
+        @pl.when(place + distance < line)
+        def _():
+            if distance:
+                across(distance).wait_send()
+                arrival(shard_ref.at[partner + 2 * distance, 0], (ys, yr), line - 1 + distance).wait_recv()
+            for lane in range(3):
+                pl.when(goes_left)(lambda: left(lane, distance).wait_send())
 
     finish(copies)
 
@@ -195,75 +208,89 @@
 
 
 def negative_kernel(
-    ndp, nneg, part_ref, sum_ref, pair_land, right_land, left_land, right_sum, left_sum, ys, yr, rs, rr, ls, lr
+    ndp, nneg, part_ref, sum_ref, pair_land, right_land, left_land, right_sum, left_sum, far_sum, far_send, far_land,
+    ys, yr, rs, rr, ls, lr,
 ):
     me_dp, me_neg = lax.axis_index("dp"), lax.axis_index("neg")
     line = ndp // 2
     place, side = me_dp // 2, lax.rem(me_dp, 2)
     partner = me_dp + 1 - 2 * side
-    cuts = part_ref.shape[1]
     greet(ndp, 1, me_dp, me_neg)
     order = sorted(range(line), key=lambda z: -abs(2 * z - line + 1))
-    steps = [(z, j) for z in order for j in range(cuts)]
     from_left, from_right = place > 0, place < line - 1
 
-    def across(z, j):
-        return link(part_ref.at[2 * z + 1 - side, j], pair_land.at[z, j], (ys, yr), z * cuts + j, "dp", partner)
-
-    def right(z, j):
-        return link(right_sum.at[z, j], right_land.at[z, j], (rs, rr), z * cuts + j, "dp", lax.rem(me_dp + 2, ndp))
-
-    def left(z, j):
-        return link(left_sum.at[z, j], left_land.at[z, j], (ls, lr), z * cuts + j, "dp", lax.rem(me_dp + ndp - 2, ndp))
-
-    for z, j in steps:
-        across(z, j).start()
-    for z, j in steps:
-        across(z, j).wait_recv()
-        own = part_ref[2 * z + side, j].astype(jnp.float32) + pair_land[z, j].astype(jnp.float32)
-
-        @pl.when(place == z)
-        def _():
-            sum_ref[j] = own
-
-        @pl.when(place == 0 if z else False)
-        def _():
-            right_sum[z, j] = own.astype(jnp.bfloat16)
-
-        @pl.when((place > 0) & (place < z))
-        def _():
-            right(z, j).wait_recv()
-            right_sum[z, j] = (own + right_land[z, j].astype(jnp.float32)).astype(jnp.bfloat16)
-
-        pl.when(place < z)(lambda: right(z, j).start())
-
-        @pl.when(place == line - 1 if z < line - 1 else False)
-        def _():
-            left_sum[z, j] = own.astype(jnp.bfloat16)
-
-        @pl.when((place < line - 1) & (place > z))
-        def _():
-            left(z, j).wait_recv()
-            left_sum[z, j] = (own + left_land[z, j].astype(jnp.float32)).astype(jnp.bfloat16)
-
-        pl.when(place > z)(lambda: left(z, j).start())
-
-    for j in range(cuts):
+    def across(z):
+        return link(part_ref.at[2 * z + 1 - side, 0], pair_land.at[z], (ys, yr), z, "dp", partner)
+
+    def right(z, lane):
+        return link(right_sum.at[z, lane], right_land.at[z, lane], (rs, rr), z * 3 + lane, "dp", lax.rem(me_dp + 2, ndp))
+
+    def left(z, lane):
+        return link(left_sum.at[z, lane], left_land.at[z, lane], (ls, lr), z * 3 + lane, "dp", lax.rem(me_dp + ndp - 2, ndp))
+
+    def total(lane):
+        return far_sum if lane == 2 else sum_ref.at[lane]
+
+    for z in order:
+        across(z).start()
+    for z in order:
+        for lane in (1, 2, 0):
+            if lane == 0:
+                across(z).wait_recv()
+                own = part_ref[2 * z + side, 0].astype(jnp.float32) + pair_land[z].astype(jnp.float32)
+            else:
+                own = part_ref[2 * z + (side if lane == 1 else 1 - side), 1].astype(jnp.float32)
+
+            @pl.when(place == z)
+            def _():
+                total(lane)[...] = own
+
+            @pl.when(place == 0 if z else False)
+            def _():
+                right_sum[z, lane] = own.astype(jnp.bfloat16)
+
+            @pl.when((place > 0) & (place < z))
+            def _():
+                right(z, lane).wait_recv()
+                right_sum[z, lane] = (own + right_land[z, lane].astype(jnp.float32)).astype(jnp.bfloat16)
+
+            pl.when(place < z)(lambda: right(z, lane).start())
+
+            @pl.when(place == line - 1 if z < line - 1 else False)
+            def _():
+                left_sum[z, lane] = own.astype(jnp.bfloat16)
+
+            @pl.when((place < line - 1) & (place > z))
+            def _():
+                left(z, lane).wait_recv()
+                left_sum[z, lane] = (own + left_land[z, lane].astype(jnp.float32)).astype(jnp.bfloat16)
+
+            pl.when(place > z)(lambda: left(z, lane).start())
+
+    second = link(far_send, far_land, (ys, yr), line, "dp", partner)
+    for lane in (2, 1, 0):
 
         @pl.when(from_left)
         def _():
-            right(place, j).wait_recv()
-            sum_ref[j] = sum_ref[j] + right_land[place, j].astype(jnp.float32)
+            right(place, lane).wait_recv()
+            total(lane)[...] = total(lane)[...] + right_land[place, lane].astype(jnp.float32)
 
         @pl.when(from_right)
         def _():
-            left(place, j).wait_recv()
-            sum_ref[j] = sum_ref[j] + left_land[place, j].astype(jnp.float32)
-
-    for z, j in steps:
-        across(z, j).wait_send()
-        pl.when(place < z)(lambda: right(z, j).wait_send())
-        pl.when(place > z)(lambda: left(z, j).wait_send())
+            left(place, lane).wait_recv()
+            total(lane)[...] = total(lane)[...] + left_land[place, lane].astype(jnp.float32)
+
+        if lane == 2:
+            far_send[...] = far_sum[...].astype(jnp.bfloat16)
+            second.start()
+
+    second.wait()
+    sum_ref[1] = sum_ref[1] + far_land[...].astype(jnp.float32)
+    for z in order:
+        across(z).wait_send()
+        for lane in range(3):
+            pl.when(place < z)(lambda: right(z, lane).wait_send())
+            pl.when(place > z)(lambda: left(z, lane).wait_send())
 
 
 def weight_kernel(
@@ -445,7 +472,7 @@
             jax.ShapeDtypeStruct((nneg,) + query_unit.shape, jnp.bfloat16),
             jax.ShapeDtypeStruct((ndp, cuts, cut_rows, width), jnp.bfloat16),
         ),
-        sems(nneg, nneg, *([ndp // 2 * cuts + cuts] * 4), *([ndp * cuts] * 2)),
+        sems(nneg, nneg, *([ndp // 2 * 3 + 3] * 4), ndp, ndp),
         [vmem, vmem],
     )(query_unit, negative_unit.reshape(cuts, cut_rows, width))
     group_unit = group_unit.reshape(-1, width)
@@ -497,7 +524,10 @@
         ndp,
         nneg,
         (jax.ShapeDtypeStruct(cut, jnp.float32),),
-        [pltpu.VMEM((line,) + cut, jnp.bfloat16)] * 5 + sems(*([line * cuts] * 6)),
+        [pltpu.VMEM((line,) + cut[1:], jnp.bfloat16)]
+        + [pltpu.VMEM((line, 3) + cut[1:], jnp.bfloat16)] * 4
+        + [pltpu.VMEM(cut[1:], kind) for kind in (jnp.float32, jnp.bfloat16, jnp.bfloat16)]
+        + sems(line + 1, line + 1, *([line * 3] * 4)),
         [vmem],
     )(negative_part.reshape((ndp,) + cut))
     negative_sum = negative_sum.reshape(negative_unit.shape)

time: 178 us -> 184 us (1.034)
  Pallas kernels: 125 us -> 131 us
    pallas_call x1, Pallas kernels: 30.1 us -> 33.4 us  [per_device(): call(negative_kernel, 2, ndp, nneg, (jax.ShapeDtypeStruct(cut, jnp.float3...]
    pallas_call x1, Pallas kernels: 30.2 us -> 33.1 us  [per_device(): call(gather_kernel, 0, ndp, nneg, (jax.ShapeDtypeStruct((nneg,) + query_u...]
where the time goes in v3:
time: 184 us
  Pallas kernels  131 us (71%)
  matrix products  36 us (20%)
  local copies, waits for them, and re-layouts  7.26 us (4%)
  other arithmetic  5.23 us (3%)
  between operations  3.81 us (2%)
    pallas_call x1, Pallas kernels, per_device(): call(weight_kernel, 3, ndp, nneg, (jax.ShapeDtypeStruct((nneg, 2) + piece...  57 us
    pallas_call x1, Pallas kernels, per_device(): call(negative_kernel, 2, ndp, nneg, (jax.ShapeDtypeStruct(cut, jnp.float3...  33.4 us
    pallas_call x1, Pallas kernels, per_device(): call(gather_kernel, 0, ndp, nneg, (jax.ShapeDtypeStruct((nneg,) + query_u...  33.1 us
    dot_general x7, matrix products, contract_rows(): lax.dot_general(left, right, (((0,), (0,)), ((), ())), preferred_element_...  17.3 us
    dot_general x3, matrix products, contract_cols(): lax.dot_general(left, right, (((1,), (1,)), ((), ())), preferred_element_...  8.77 us
    pallas_call x1, Pallas kernels, per_device(): call(query_kernel, 1, ndp, nneg, (jax.ShapeDtypeStruct((own_rows, width),...  8.02 us
    unnamed x88, local copies, waits for them, and re-layouts  5.03 us

profile of v3, /device:TPU:0, one launch (start us, length us, event | category | flops | bytes accessed | tf_op | source)
XLA Modules:
  0.0 183.8 jit_solution(528320557504236423)
XLA Ops:
  0.6 0.0 copy-start
  0.6 1.1 constant_dynamic-update-slice_fusion.1
  1.7 1.1 constant_dynamic-update-slice_fusion
  2.8 2.9 %multiply_convert_fusion.1 = (bf16[768,1024]{1,0:T(8,128)(2,1)S(1)}, f32[768,1024]{1,0:T(8,128)}) fusion(bf16[768,512]{1,0:T(8,128)(2,1)S(1)} %constant_dynamic-update-slice_fusion, bf16[512,1024]{1,0:T(8,128)(2,1)S(1)} %copy-done), kind=kOutput, calls=%fused_computation.6 | convolution fusion | flops 809238528 | bytes 6553600 | tf_op jit(solution)/shard_map/dot_general | solution.py:32
  5.7 2.3 %multiply_convert_fusion.3 = (bf16[768,512]{1,0:T(8,128)(2,1)S(1)}, f32[768,512]{1,0:T(8,128)}) fusion(bf16[768,1024]{1,0:T(8,128)(2,1)S(1)} %get-tuple-element.50, bf16[1024,512]{1,0:T(8,128)(2,1)S(1)} %copy-done.28), kind=kOutput, calls=%fused_computation.9 | convolution fusion | flops 807272448 | bytes 4980736 | tf_op jit(solution)/shard_map/dot_general | solution.py:34
  8.0 0.4 multiply_reduce_fusion.1
  8.5 0.4 copy-done.9
  8.9 0.2 multiply_convert_fusion.5
  9.1 0.4 copy-done.3
  9.5 0.0 copy-done.15
  9.5 0.4 fusion.19
  10.1 1.3 multiply_convert_fusion.6
  11.3 0.3 multiply_reduce_fusion.3
  11.6 0.4 copy-done.7
  12.0 0.1 copy.23
  12.2 0.6 broadcast_multiply_fusion.1
  12.8 0.2 fusion.11
  13.0 33.1 %shard_map.180 = (bf16[4,256,256]{2,1,0:T(8,128)(2,1)S(1)}, bf16[8,2,256,256]{3,2,1,0:T(8,128)(2,1)S(1)}) custom-call(bf16[256,256]{1,0:T(8,128)(2,1)S(1)} %get-tuple-element.22.query_ref, bf16[2,256,256]{2,1,0:T(8,128)(2,1)S(1)} %bitcast.59), custom_call_target="tpu_custom_call" | custom-call | tf_op jit(solution)/shard_map/pallas_call | solution.py:466
  46.1 5.1 %fusion = (f32[1024]{0:T(1024)S(1)}, bf16[1024,4096]{1,0:T(8,128)(2,1)S(1)}) fusion(f32[4096]{0:T(1024)S(1)} %convert_log_fusion, s32[4096]{0:T(1024)S(1)} %copy-done.30, s32[1024]{0:T(1024)S(1)} %copy-done.31, bf16[1024,256]{1,0:T(8,128)(2,1)S(1)} %bitcast.69, bf16[4096,256]{1,0:T(8,128)(2,1)S(1)} %bitcast.67), kind=kOutput, calls=%fused_computation.1 | convolution fusion | flops 2172648448 | bytes 11051008 | tf_op jit(solution)/shard_map/dot_general | solution.py:26
  51.3 2.3 %convolution_convert_fusion.5 = bf16[1024,256]{1,0:T(8,128)(2,1)S(1)} fusion(bf16[1024,4096]{1,0:T(8,128)(2,1)S(1)} %get-tuple-element.24, bf16[4096,256]{1,0:T(8,128)(2,1)S(1)} %bitcast.68), kind=kOutput, calls=%fused_computation.16 | convolution fusion | flops 2147745792 | bytes 11010048 | tf_op jit(solution)/shard_map/dot_general | solution.py:494
  53.6 0.9 copy-done.32
  54.5 0.1 add_dynamic-update-slice_fusion
  54.7 8.0 %shard_map.181 = (f32[256,256]{1,0:T(8,128)S(1)}, f32[8,128]{1,0:T(8,128)S(1)}) custom-call(bf16[4,256,256]{2,1,0:T(8,128)(2,1)S(1)} %bitcast.63, f32[8,128]{1,0:T(8,128)S(1)} %bitcast.64), custom_call_target="tpu_custom_call" | custom-call | tf_op jit(solution)/shard_map/pallas_call | solution.py:496
  62.7 5.9 %convolution_convert_fusion = bf16[4096,256]{1,0:T(8,128)(2,1)S(1)} fusion(bf16[1024,4096]{1,0:T(8,128)(2,1)} %copy-done.32, bf16[1024,256]{1,0:T(8,128)(2,1)S(1)} %bitcast.70, f32[1024]{0:T(1024)S(1)} %bitcast.65), kind=kOutput, calls=%fused_computation.3 | convolution fusion | flops 2149318656 | bytes 11014144 | tf_op jit(solution)/shard_map/dot_general | solution.py:20
  68.7 33.4 %shard_map.182 = f32[2,256,256]{2,1,0:T(8,128)S(1)} custom-call(bf16[8,2,256,256]{3,2,1,0:T(8,128)(2,1)S(1)} %bitcast.58), custom_call_target="tpu_custom_call" | custom-call | tf_op jit(solution)/shard_map/pallas_call | solution.py:521
  102.1 0.7 subtract_reduce_fusion
  102.8 0.2 fusion.10
  103.1 0.2 multiply_reduce_fusion
  103.3 0.4 subtract_convert_fusion
  103.7 1.6 multiply_convert_fusion.2
  105.4 5.5 %convolution_convert_fusion.2 = bf16[512,1024]{1,0:T(8,128)(2,1)} fusion(bf16[768,512]{1,0:T(8,128)(2,1)S(1)} %copy-done.20, f32[768,1024]{1,0:T(8,128)} %get-tuple-element.51, bf16[768,512]{1,0:T(8,128)(2,1)} %multiply_convert_fusion.2, bf16[1024,512]{1,0:T(8,128)(2,1)} %param.24), kind=kOutput, calls=%fused_computation.12 | convolution fusion | flops 1618214912 | bytes 6815744 | tf_op jit(solution)/shard_map/dot_general | solution.py:20
  110.9 0.2 subtract_convert_fusion.1
  111.2 2.1 %fusion.3 = bf16[256,512]{1,0:T(8,128)(2,1)} fusion(bf16[256,256]{1,0:T(8,128)(2,1)S(1)} %subtract_convert_fusion.1, bf16[512,256]{1,0:T(8,128)(2,1)S(1)} %copy-done.18, f32[256,512]{1,0:T(8,128)} %get-tuple-element.49), kind=kOutput, calls=%fused_computation.21 | convolution fusion | flops 68288512 | bytes 1179648 | tf_op jit(solution)/shard_map/dot_general | solution.py:26
  113.2 2.6 %convolution_convert_fusion.4 = bf16[1024,512]{0,1:T(8,128)(2,1)S(1)} fusion(bf16[256,512]{1,0:T(8,128)(2,1)S(1)} %copy-done.16, bf16[256,512]{1,0:T(8,128)(2,1)} %fusion.3, bf16[1024,512]{1,0:T(8,128)(2,1)} %param.21, f32[256,1024]{1,0:T(8,128)} %copy-done.4), kind=kOutput, calls=%fused_computation.14 | convolution fusion | flops 539754496 | bytes 3670016 | tf_op jit(solution)/shard_map/dot_general | solution.py:20
  116.1 1.6 convolution_convert_fusion.3
  117.8 0.3 convolution_convert_fusion.7
  118.2 0.8 copy-done.34
  119.0 0.2 copy-done.35
  119.2 1.0 convolution_convert_fusion.1
  120.3 0.0 copy-done.10
  120.4 0.1 copy-done.12
  120.5 0.4 convolution_convert_fusion.6
  120.9 0.3 copy.28
  121.2 57.0 %shard_map.183 = (bf16[4,2,144,256]{3,2,1,0:T(8,128)(2,1)S(1)}, f32[8,128]{1,0:T(8,128)S(1)}) custom-call(bf16[4,8,2,144,256]{4,3,2,1,0:T(8,128)(2,1)S(1)} %bitcast.57, f32[1]{0:T(128)} %bitcast.18.loss_ref), custom_call_target="tpu_custom_call" | custom-call | tf_op jit(solution)/shard_map/pallas_call | solution.py:549
  178.2 0.6 fusion.18
  179.6 0.7 convert_multiply_fusion.7
  180.3 0.9 convert_multiply_fusion.3
  181.2 0.8 convert_multiply_fusion.4
  (85 shorter events, 0.8 us)
Async XLA Ops:
  0.6 2.2 %copy-start = (bf16[512,1024]{1,0:T(8,128)(2,1)S(1)}, bf16[512,1024]{1,0:T(8,128)(2,1)}, u32[]{:S(2)}) copy-start(bf16[512,1024]{1,0:T(8,128)(2,1)} %param.23) | copy-start | bytes 3145732
  2.8 2.9 %copy-start.19 = (bf16[768,512]{1,0:T(8,128)(2,1)}, bf16[768,512]{1,0:T(8,128)(2,1)S(1)}, u32[]{:S(2)}) copy-start(bf16[768,512]{1,0:T(8,128)(2,1)S(1)} %constant_dynamic-update-slice_fusion) | copy-start | bytes 2359300
  2.8 2.9 %copy-start.28 = (bf16[1024,512]{1,0:T(8,128)(2,1)S(1)}, bf16[1024,512]{1,0:T(8,128)(2,1)}, u32[]{:S(2)}) copy-start(bf16[1024,512]{1,0:T(8,128)(2,1)} %param.24) | copy-start | bytes 3145732
  5.7 2.3 %copy-start.33 = (bf16[768,1024]{1,0:T(8,128)(2,1)}, bf16[768,1024]{1,0:T(8,128)(2,1)S(1)}, u32[]{:S(2)}) copy-start(bf16[768,1024]{1,0:T(8,128)(2,1)S(1)} %get-tuple-element.50) | copy-start | bytes 4718596
  5.7 2.3 %copy-start.13 = (bf16[512,256]{1,0:T(8,128)(2,1)S(1)}, bf16[512,256]{1,0:T(8,128)(2,1)}, u32[]{:S(2)}) copy-start(bf16[512,256]{1,0:T(8,128)(2,1)} %param.25) | copy-start | bytes 786436
  8.0 0.9 copy-start.9
  8.0 1.5 copy-start.3
  8.0 1.5 copy-start.15
  8.0 2.0 %copy-start.29 = (bf16[1024,512]{1,0:T(8,128)(2,1)S(1)}, bf16[1024,512]{1,0:T(8,128)(2,1)}, u32[]{:S(2)}) copy-start(bf16[1024,512]{1,0:T(8,128)(2,1)} %param.21) | copy-start | bytes 3145732
  9.5 3.4 %copy-start.1 = (bf16[768,256]{1,0:T(8,128)(2,1)}, bf16[768,256]{1,0:T(8,128)(2,1)S(1)}, u32[]{:S(2)}) copy-start(bf16[768,256]{1,0:T(8,128)(2,1)S(1)} %multiply_convert_fusion.5) | copy-start | bytes 1179652
  10.0 1.3 copy-start.4
  10.0 1.3 copy-start.17
  10.0 36.1 %copy-start.21 = (s32[4096]{0:T(1024)S(1)}, s32[4096]{0:T(1024)}, u32[]{:S(2)}) copy-start(s32[4096]{0:T(1024)} %param.19) | copy-start | bytes 49156
  10.0 36.1 %copy-start.30 = (s32[4096]{0:T(1024)S(1)}, s32[4096]{0:T(1024)}, u32[]{:S(2)}) copy-start(s32[4096]{0:T(1024)} %param.18) | copy-start | bytes 49156
  10.0 36.1 %copy-start.31 = (s32[1024]{0:T(1024)S(1)}, s32[1024]{0:T(1024)}, u32[]{:S(2)}) copy-start(s32[1024]{0:T(1024)} %param.16) | copy-start | bytes 12292
  11.3 0.7 copy-start.7
  51.2 3.3 %copy-start.32 = (bf16[1024,4096]{1,0:T(8,128)(2,1)}, bf16[1024,4096]{1,0:T(8,128)(2,1)S(1)}, u32[]{:S(2)}) copy-start(bf16[1024,4096]{1,0:T(8,128)(2,1)S(1)} %get-tuple-element.24) | copy-start | bytes 25165828
  51.3 3.3 %copy-start.24 = (s32[256]{0:T(256)S(1)}, s32[256]{0:T(256)}, u32[]{:S(2)}) copy-start(s32[256]{0:T(256)} %param.17) | copy-start | bytes 3076
  68.7 33.5 %copy-start.25 = (s32[256]{0:T(256)S(1)}, s32[256]{0:T(256)}, u32[]{:S(2)}) copy-start(s32[256]{0:T(256)} %param.17) | copy-start | bytes 3076
  68.7 34.2 %copy-start.2 = (bf16[768,256]{1,0:T(8,128)(2,1)S(1)}, bf16[768,256]{1,0:T(8,128)(2,1)}, u32[]{:S(2)}) copy-start(bf16[768,256]{1,0:T(8,128)(2,1)} %copy-done.1) | copy-start | bytes 1179652
  102.1 1.6 copy-start.14
  102.1 1.6 copy-start.36
  102.8 2.5 %copy-start.22 = (f32[256]{0:T(256)}, f32[256]{0:T(256)S(1)}, u32[]{:S(2)}) copy-start(f32[256]{0:T(256)S(1)} %divide_add_fusion) | copy-start | bytes 3076
  103.7 1.7 copy-start.11
  103.7 1.6 copy-start.20
  105.3 5.6 %copy-start.23 = (f32[256]{0:T(256)S(1)}, f32[256]{0:T(256)}, u32[]{:S(2)}) copy-start(f32[256]{0:T(256)} %copy-done.22) | copy-start | bytes 3076
  105.3 5.6 %copy-start.26 = (f32[256]{0:T(256)S(1)}, f32[256]{0:T(256)}, u32[]{:S(2)}) copy-start(f32[256]{0:T(256)} %get-tuple-element.45) | copy-start | bytes 3076
  105.3 5.6 %copy-start.27 = (f32[256]{0:T(256)S(1)}, f32[256]{0:T(256)}, u32[]{:S(2)}) copy-start(f32[256]{0:T(256)} %get-tuple-element.46) | copy-start | bytes 3076
  105.3 5.8 %copy-start.18 = (bf16[512,256]{1,0:T(8,128)(2,1)S(1)}, bf16[512,256]{1,0:T(8,128)(2,1)}, u32[]{:S(2)}) copy-start(bf16[512,256]{1,0:T(8,128)(2,1)} %param.22) | copy-start | bytes 786436
  110.9 2.3 %copy-start.16 = (bf16[256,512]{1,0:T(8,128)(2,1)S(1)}, bf16[256,512]{1,0:T(8,128)(2,1)}, u32[]{:S(2)}) copy-start(bf16[256,512]{1,0:T(8,128)(2,1)} %param.13) | copy-start | bytes 786436
  113.2 2.8 %copy-start.5 = (f32[256,1024]{1,0:T(8,128)S(1)}, f32[256,1024]{1,0:T(8,128)}, u32[]{:S(2)}) copy-start(f32[256,1024]{1,0:T(8,128)} %copy-done.4) | copy-start | bytes 3145732
  116.0 1.7 copy-start.8
  116.1 2.0 %copy-start.6 = (bf16[512,1024]{1,0:T(8,128)(2,1)S(1)}, bf16[512,1024]{1,0:T(8,128)(2,1)}, u32[]{:S(2)}) copy-start(bf16[512,1024]{1,0:T(8,128)(2,1)} %convolution_convert_fusion.2) | copy-start | bytes 3145732
  117.6 1.4 copy-start.34
  117.6 1.6 copy-start.35
  119.2 1.1 copy-start.10
  119.2 1.2 copy-start.12

commit v4 on v2

--- a/solution.py
+++ b/solution.py
@@ -434,7 +434,7 @@
     negative_unit = item_unit[own_rows:]
     ndp, nneg = lax.axis_size("dp"), lax.axis_size("neg")
     width = query_unit.shape[1]
-    cuts = 2
+    cuts = 4
     cut_rows = negative_unit.shape[0] // cuts
     group_unit, shard_unit = call(
         gather_kernel,

time: 178 us -> 177 us (level)
  no operation moved by 1% of the time
where the time goes in v4:
time: 177 us; the launch traced here: 176 us
  Pallas kernels  124 us (70%)
  matrix products  36 us (20%)
  local copies, waits for them, and re-layouts  7.26 us (4%)
  other arithmetic  5.3 us (3%)
  between operations  3.82 us (2%)
    pallas_call x1, Pallas kernels, per_device(): call(weight_kernel, 3, ndp, nneg, (jax.ShapeDtypeStruct((nneg, 2) + piece...  55.8 us
    pallas_call x1, Pallas kernels, per_device(): call(gather_kernel, 0, ndp, nneg, (jax.ShapeDtypeStruct((nneg,) + query_u...  30.9 us
    pallas_call x1, Pallas kernels, per_device(): call(negative_kernel, 2, ndp, nneg, (jax.ShapeDtypeStruct(cut, jnp.float3...  29.1 us
    dot_general x7, matrix products, contract_rows(): lax.dot_general(left, right, (((0,), (0,)), ((), ())), preferred_element_...  17.3 us
    dot_general x3, matrix products, contract_cols(): lax.dot_general(left, right, (((1,), (1,)), ((), ())), preferred_element_...  8.77 us
    pallas_call x1, Pallas kernels, per_device(): call(query_kernel, 1, ndp, nneg, (jax.ShapeDtypeStruct((own_rows, width),...  8.04 us
    unnamed x88, local copies, waits for them, and re-layouts  5.03 us
    dot_general x2, matrix products, tower_forward(): second_pre = jnp.dot(first_act, second, preferred_element_type=jnp.float32)  3.55 us

profile of v4, /device:TPU:0, one launch (start us, length us, event | category | flops | bytes accessed | tf_op | source)
XLA Modules:
  0.0 176.3 jit_solution(3404385544018689303)
XLA Ops:
  0.6 0.0 copy-start
  0.6 1.1 constant_dynamic-update-slice_fusion.1
  1.7 1.1 constant_dynamic-update-slice_fusion
  2.8 2.9 %multiply_convert_fusion.1 = (bf16[768,1024]{1,0:T(8,128)(2,1)S(1)}, f32[768,1024]{1,0:T(8,128)}) fusion(bf16[768,512]{1,0:T(8,128)(2,1)S(1)} %constant_dynamic-update-slice_fusion, bf16[512,1024]{1,0:T(8,128)(2,1)S(1)} %copy-done), kind=kOutput, calls=%fused_computation.6 | convolution fusion | flops 809238528 | bytes 6553600 | tf_op jit(solution)/shard_map/dot_general | solution.py:32
  5.7 2.3 %multiply_convert_fusion.3 = (bf16[768,512]{1,0:T(8,128)(2,1)S(1)}, f32[768,512]{1,0:T(8,128)}) fusion(bf16[768,1024]{1,0:T(8,128)(2,1)S(1)} %get-tuple-element.50, bf16[1024,512]{1,0:T(8,128)(2,1)S(1)} %copy-done.28), kind=kOutput, calls=%fused_computation.9 | convolution fusion | flops 807272448 | bytes 4980736 | tf_op jit(solution)/shard_map/dot_general | solution.py:34
  8.0 0.4 multiply_reduce_fusion.1
  8.5 0.4 copy-done.9
  8.9 0.2 multiply_convert_fusion.5
  9.1 0.4 copy-done.3
  9.5 0.0 copy-done.15
  9.5 0.4 fusion.19
  10.1 1.3 multiply_convert_fusion.6
  11.3 0.3 multiply_reduce_fusion.3
  11.6 0.4 copy-done.7
  12.0 0.1 copy.23
  12.2 0.6 broadcast_multiply_fusion.1
  12.8 0.2 fusion.11
  13.0 30.9 %shard_map.180 = (bf16[4,256,256]{2,1,0:T(8,128)(2,1)S(1)}, bf16[8,4,128,256]{3,2,1,0:T(8,128)(2,1)S(1)}) custom-call(bf16[256,256]{1,0:T(8,128)(2,1)S(1)} %get-tuple-element.22.query_ref, bf16[4,128,256]{2,1,0:T(8,128)(2,1)S(1)} %bitcast.59), custom_call_target="tpu_custom_call" | custom-call | tf_op jit(solution)/shard_map/pallas_call | solution.py:439
  43.9 5.1 %fusion = (f32[1024]{0:T(1024)S(1)}, bf16[1024,4096]{1,0:T(8,128)(2,1)S(1)}) fusion(f32[4096]{0:T(1024)S(1)} %convert_log_fusion, s32[4096]{0:T(1024)S(1)} %copy-done.30, s32[1024]{0:T(1024)S(1)} %copy-done.31, bf16[1024,256]{1,0:T(8,128)(2,1)S(1)} %bitcast.69, bf16[4096,256]{1,0:T(8,128)(2,1)S(1)} %bitcast.67), kind=kOutput, calls=%fused_computation.1 | convolution fusion | flops 2172648448 | bytes 11051008 | tf_op jit(solution)/shard_map/dot_general | solution.py:26
  49.0 2.3 %convolution_convert_fusion.5 = bf16[1024,256]{1,0:T(8,128)(2,1)S(1)} fusion(bf16[1024,4096]{1,0:T(8,128)(2,1)S(1)} %get-tuple-element.24, bf16[4096,256]{1,0:T(8,128)(2,1)S(1)} %bitcast.68), kind=kOutput, calls=%fused_computation.16 | convolution fusion | flops 2147745792 | bytes 11010048 | tf_op jit(solution)/shard_map/dot_general | solution.py:467
  51.4 0.9 copy-done.32
  52.3 0.2 add_dynamic-update-slice_fusion
  52.5 8.0 %shard_map.181 = (f32[256,256]{1,0:T(8,128)S(1)}, f32[8,128]{1,0:T(8,128)S(1)}) custom-call(bf16[4,256,256]{2,1,0:T(8,128)(2,1)S(1)} %bitcast.63, f32[8,128]{1,0:T(8,128)S(1)} %bitcast.64), custom_call_target="tpu_custom_call" | custom-call | tf_op jit(solution)/shard_map/pallas_call | solution.py:469
  60.6 5.9 %convolution_convert_fusion = bf16[4096,256]{1,0:T(8,128)(2,1)S(1)} fusion(bf16[1024,4096]{1,0:T(8,128)(2,1)} %copy-done.32, bf16[1024,256]{1,0:T(8,128)(2,1)S(1)} %bitcast.70, f32[1024]{0:T(1024)S(1)} %bitcast.65), kind=kOutput, calls=%fused_computation.3 | convolution fusion | flops 2149318656 | bytes 11014144 | tf_op jit(solution)/shard_map/dot_general | solution.py:20
  66.6 29.1 %shard_map.182 = f32[4,128,256]{2,1,0:T(8,128)S(1)} custom-call(bf16[8,4,128,256]{3,2,1,0:T(8,128)(2,1)S(1)} %bitcast.58), custom_call_target="tpu_custom_call" | custom-call | tf_op jit(solution)/shard_map/pallas_call | solution.py:494
  95.8 0.7 subtract_reduce_fusion
  96.5 0.2 fusion.10
  96.7 0.2 multiply_reduce_fusion
  96.9 0.4 subtract_convert_fusion
  97.3 1.6 multiply_convert_fusion.2
  99.0 5.5 %convolution_convert_fusion.2 = bf16[512,1024]{1,0:T(8,128)(2,1)} fusion(bf16[768,512]{1,0:T(8,128)(2,1)S(1)} %copy-done.20, f32[768,1024]{1,0:T(8,128)} %get-tuple-element.51, bf16[768,512]{1,0:T(8,128)(2,1)} %multiply_convert_fusion.2, bf16[1024,512]{1,0:T(8,128)(2,1)} %param.24), kind=kOutput, calls=%fused_computation.12 | convolution fusion | flops 1618214912 | bytes 6815744 | tf_op jit(solution)/shard_map/dot_general | solution.py:20
  104.5 0.2 subtract_convert_fusion.1
  104.8 2.1 %fusion.3 = bf16[256,512]{1,0:T(8,128)(2,1)} fusion(bf16[256,256]{1,0:T(8,128)(2,1)S(1)} %subtract_convert_fusion.1, bf16[512,256]{1,0:T(8,128)(2,1)S(1)} %copy-done.18, f32[256,512]{1,0:T(8,128)} %get-tuple-element.49), kind=kOutput, calls=%fused_computation.21 | convolution fusion | flops 68288512 | bytes 1179648 | tf_op jit(solution)/shard_map/dot_general | solution.py:26
  106.9 2.6 %convolution_convert_fusion.4 = bf16[1024,512]{0,1:T(8,128)(2,1)S(1)} fusion(bf16[256,512]{1,0:T(8,128)(2,1)S(1)} %copy-done.16, bf16[256,512]{1,0:T(8,128)(2,1)} %fusion.3, bf16[1024,512]{1,0:T(8,128)(2,1)} %param.21, f32[256,1024]{1,0:T(8,128)} %copy-done.4), kind=kOutput, calls=%fused_computation.14 | convolution fusion | flops 539754496 | bytes 3670016 | tf_op jit(solution)/shard_map/dot_general | solution.py:20
  109.7 1.6 convolution_convert_fusion.3
  111.4 0.3 convolution_convert_fusion.7
  111.9 0.8 copy-done.34
  112.7 0.2 copy-done.35
  112.9 1.0 convolution_convert_fusion.1
  114.0 0.0 copy-done.10
  114.0 0.1 copy-done.12
  114.1 0.4 convolution_convert_fusion.6
  114.5 0.3 copy.28
  114.8 55.8 %shard_map.183 = (bf16[4,2,144,256]{3,2,1,0:T(8,128)(2,1)S(1)}, f32[8,128]{1,0:T(8,128)S(1)}) custom-call(bf16[4,8,2,144,256]{4,3,2,1,0:T(8,128)(2,1)S(1)} %bitcast.57, f32[1]{0:T(128)} %bitcast.18.loss_ref), custom_call_target="tpu_custom_call" | custom-call | tf_op jit(solution)/shard_map/pallas_call | solution.py:519
  170.7 0.6 fusion.18
  172.1 0.7 convert_multiply_fusion.7
  172.7 0.9 convert_multiply_fusion.3
  173.6 0.8 convert_multiply_fusion.4
  (85 shorter events, 0.8 us)
Async XLA Ops:
  0.6 2.2 %copy-start = (bf16[512,1024]{1,0:T(8,128)(2,1)S(1)}, bf16[512,1024]{1,0:T(8,128)(2,1)}, u32[]{:S(2)}) copy-start(bf16[512,1024]{1,0:T(8,128)(2,1)} %param.23) | copy-start | bytes 3145732
  2.8 2.9 %copy-start.19 = (bf16[768,512]{1,0:T(8,128)(2,1)}, bf16[768,512]{1,0:T(8,128)(2,1)S(1)}, u32[]{:S(2)}) copy-start(bf16[768,512]{1,0:T(8,128)(2,1)S(1)} %constant_dynamic-update-slice_fusion) | copy-start | bytes 2359300
  2.8 2.9 %copy-start.28 = (bf16[1024,512]{1,0:T(8,128)(2,1)S(1)}, bf16[1024,512]{1,0:T(8,128)(2,1)}, u32[]{:S(2)}) copy-start(bf16[1024,512]{1,0:T(8,128)(2,1)} %param.24) | copy-start | bytes 3145732
  5.7 2.3 %copy-start.33 = (bf16[768,1024]{1,0:T(8,128)(2,1)}, bf16[768,1024]{1,0:T(8,128)(2,1)S(1)}, u32[]{:S(2)}) copy-start(bf16[768,1024]{1,0:T(8,128)(2,1)S(1)} %get-tuple-element.50) | copy-start | bytes 4718596
  5.7 2.3 %copy-start.13 = (bf16[512,256]{1,0:T(8,128)(2,1)S(1)}, bf16[512,256]{1,0:T(8,128)(2,1)}, u32[]{:S(2)}) copy-start(bf16[512,256]{1,0:T(8,128)(2,1)} %param.25) | copy-start | bytes 786436
  8.0 0.9 copy-start.9
  8.0 1.5 copy-start.3
  8.0 1.5 copy-start.15
  8.0 2.0 %copy-start.29 = (bf16[1024,512]{1,0:T(8,128)(2,1)S(1)}, bf16[1024,512]{1,0:T(8,128)(2,1)}, u32[]{:S(2)}) copy-start(bf16[1024,512]{1,0:T(8,128)(2,1)} %param.21) | copy-start | bytes 3145732
  9.5 3.4 %copy-start.1 = (bf16[768,256]{1,0:T(8,128)(2,1)}, bf16[768,256]{1,0:T(8,128)(2,1)S(1)}, u32[]{:S(2)}) copy-start(bf16[768,256]{1,0:T(8,128)(2,1)S(1)} %multiply_convert_fusion.5) | copy-start | bytes 1179652
  10.0 1.3 copy-start.4
  10.0 1.3 copy-start.17
  10.0 33.8 %copy-start.21 = (s32[4096]{0:T(1024)S(1)}, s32[4096]{0:T(1024)}, u32[]{:S(2)}) copy-start(s32[4096]{0:T(1024)} %param.19) | copy-start | bytes 49156
  10.0 33.9 %copy-start.30 = (s32[4096]{0:T(1024)S(1)}, s32[4096]{0:T(1024)}, u32[]{:S(2)}) copy-start(s32[4096]{0:T(1024)} %param.18) | copy-start | bytes 49156
  10.0 33.9 %copy-start.31 = (s32[1024]{0:T(1024)S(1)}, s32[1024]{0:T(1024)}, u32[]{:S(2)}) copy-start(s32[1024]{0:T(1024)} %param.16) | copy-start | bytes 12292
  11.3 0.7 copy-start.7
  49.0 3.3 %copy-start.32 = (bf16[1024,4096]{1,0:T(8,128)(2,1)}, bf16[1024,4096]{1,0:T(8,128)(2,1)S(1)}, u32[]{:S(2)}) copy-start(bf16[1024,4096]{1,0:T(8,128)(2,1)S(1)} %get-tuple-element.24) | copy-start | bytes 25165828
  49.0 3.3 %copy-start.24 = (s32[256]{0:T(256)S(1)}, s32[256]{0:T(256)}, u32[]{:S(2)}) copy-start(s32[256]{0:T(256)} %param.17) | copy-start | bytes 3076
  66.5 29.2 %copy-start.25 = (s32[256]{0:T(256)S(1)}, s32[256]{0:T(256)}, u32[]{:S(2)}) copy-start(s32[256]{0:T(256)} %param.17) | copy-start | bytes 3076
  66.5 29.9 %copy-start.2 = (bf16[768,256]{1,0:T(8,128)(2,1)S(1)}, bf16[768,256]{1,0:T(8,128)(2,1)}, u32[]{:S(2)}) copy-start(bf16[768,256]{1,0:T(8,128)(2,1)} %copy-done.1) | copy-start | bytes 1179652
  95.7 1.6 copy-start.14
  95.7 1.6 copy-start.36
  96.4 2.5 %copy-start.22 = (f32[256]{0:T(256)}, f32[256]{0:T(256)S(1)}, u32[]{:S(2)}) copy-start(f32[256]{0:T(256)S(1)} %divide_add_fusion) | copy-start | bytes 3076
  97.3 1.7 copy-start.11
  97.3 1.6 copy-start.20
  98.9 5.6 %copy-start.23 = (f32[256]{0:T(256)S(1)}, f32[256]{0:T(256)}, u32[]{:S(2)}) copy-start(f32[256]{0:T(256)} %copy-done.22) | copy-start | bytes 3076
  98.9 5.6 %copy-start.26 = (f32[256]{0:T(256)S(1)}, f32[256]{0:T(256)}, u32[]{:S(2)}) copy-start(f32[256]{0:T(256)} %get-tuple-element.45) | copy-start | bytes 3076
  99.0 5.6 %copy-start.27 = (f32[256]{0:T(256)S(1)}, f32[256]{0:T(256)}, u32[]{:S(2)}) copy-start(f32[256]{0:T(256)} %get-tuple-element.46) | copy-start | bytes 3076
  99.0 5.8 %copy-start.18 = (bf16[512,256]{1,0:T(8,128)(2,1)S(1)}, bf16[512,256]{1,0:T(8,128)(2,1)}, u32[]{:S(2)}) copy-start(bf16[512,256]{1,0:T(8,128)(2,1)} %param.22) | copy-start | bytes 786436
  104.5 2.3 %copy-start.16 = (bf16[256,512]{1,0:T(8,128)(2,1)S(1)}, bf16[256,512]{1,0:T(8,128)(2,1)}, u32[]{:S(2)}) copy-start(bf16[256,512]{1,0:T(8,128)(2,1)} %param.13) | copy-start | bytes 786436
  106.8 2.8 %copy-start.5 = (f32[256,1024]{1,0:T(8,128)S(1)}, f32[256,1024]{1,0:T(8,128)}, u32[]{:S(2)}) copy-start(f32[256,1024]{1,0:T(8,128)} %copy-done.4) | copy-start | bytes 3145732
  109.7 1.7 copy-start.8
  109.7 2.0 %copy-start.6 = (bf16[512,1024]{1,0:T(8,128)(2,1)S(1)}, bf16[512,1024]{1,0:T(8,128)(2,1)}, u32[]{:S(2)}) copy-start(bf16[512,1024]{1,0:T(8,128)(2,1)} %convolution_convert_fusion.2) | copy-start | bytes 3145732
  111.2 1.4 copy-start.34
  111.3 1.6 copy-start.35
  112.9 1.1 copy-start.10
  112.9 1.2 copy-start.12
